TPU v7x, 128 devices: a whole 4x4x4 slice. The times are simulated.
128 devices in a mesh: seq: 16 (over x, z), head: 8 (over y, core).
Axes of the slice: x: 4, y: 4, z: 4, core: 2. Of those that a mesh axis runs over, the one named last changes fastest.
Arguments:
- latent: float32 [4096, 128], P('seq'), may hold values from -6 to 6
- w_in: bfloat16 [128, 3072], replicated, may hold values from -0.5 to 0.5
- w_query: bfloat16 [3072, 3072], P(None, 'head'), may hold values from -0.109375 to 0.109375
- w_key: bfloat16 [3072, 3072], P(None, 'head'), may hold values from -0.109375 to 0.109375
- w_value: bfloat16 [3072, 3072], P(None, 'head'), may hold values from -0.109375 to 0.109375
- w_attn_out: bfloat16 [3072, 3072], P('head'), may hold values from -0.109375 to 0.109375
- w_up: bfloat16 [3072, 12288], P('seq', 'head'), may hold values from -0.109375 to 0.109375
- w_down: bfloat16 [12288, 3072], P('head', 'seq'), may hold values from -0.0546875 to 0.0546875
- w_final: bfloat16 [3072, 256], replicated, may hold values from -0.109375 to 0.109375
- gain_attn: float32 [3072], replicated, may hold values from 0.5 to 1.5
- gain_mlp: float32 [3072], replicated, may hold values from 0.5 to 1.5
- gain_final: float32 [3072], replicated, may hold values from 0.5 to 1.5
Outputs:
- restored: float32 [4096, 128], P('seq')
All inputs are finite; a program needn't handle non-finite values.
Results may differ from a plain program's by a relative error of at most 0.013.
Values may be sent and summed in bfloat16 or wider, within the bound.
A program may use at most 192 MiB of HBM per device.

v0:
```python
import functools

import jax
import jax.numpy as jnp
from jax import lax
from jax.experimental import pallas as pl
from jax.experimental.pallas import tpu as pltpu
from jax.sharding import PartitionSpec as P

D = 3072
HALF = D // 2
HEAD_DIM = 128
C = 128
ITERS = 2
EPSILON = 1e-05
KEY_BLOCK = 512
BF16 = jnp.bfloat16
F32 = jnp.float32


def split_two(value):
    high = value.astype(BF16)
    return high, (value - high.astype(F32)).astype(BF16)


def dot(left, right):
    return jnp.dot(left, right, preferred_element_type=F32)


def dot_t(left, right):
    return lax.dot_general(left, right, (((1,), (1,)), ((), ())), preferred_element_type=F32)


def layer_norm(stream, gain):
    center = stream - jnp.mean(stream, axis=-1, keepdims=True)
    spread = jnp.mean(center * center, axis=-1, keepdims=True)
    return center * lax.rsqrt(spread + EPSILON) * gain


def frequencies():
    return jnp.exp(-jnp.log(10000.0) * 2.0 * jnp.arange(HALF).astype(F32) / D)


MESH = pl.DeviceIdType.MESH


def seat():
    head = lax.axis_index("head")
    return lax.axis_index("seq"), lax.div(head, 2), lax.rem(head, 2)


def plus(y, by):
    return lax.rem(y + by, 4)


def greet(targets):
    barrier = pltpu.get_barrier_semaphore()
    for target in targets:
        pl.semaphore_signal(barrier, inc=1, device_id=target, device_id_type=MESH)
    pl.semaphore_wait(barrier, len(targets))


def greet_all(devices, meanwhile=lambda: None):
    seq, y, c = seat()
    place = seq * 4 + y
    barrier = pltpu.get_barrier_semaphore()
    pl.semaphore_signal(barrier, inc=1, device_id={"head": 2 * y + 1 - c}, device_id_type=MESH)

    @pl.loop(1, devices)
    def _(k):
        other = lax.rem(place + k, devices)
        pl.semaphore_signal(
            barrier, inc=1,
            device_id={"seq": lax.div(other, 4), "head": 2 * lax.rem(other, 4) + c},
            device_id_type=MESH,
        )

    meanwhile()
    pl.semaphore_wait(barrier, devices)


def spread(buffer, send, recv):
    seq, y, c = seat()
    devices = buffer.shape[0]
    place = seq * 4 + y
    partner = {"head": 2 * y + 1 - c}
    whole = buffer.at[pl.ds(0, devices - 1), c]
    arrived = pltpu.make_async_remote_copy(
        src_ref=whole, dst_ref=whole, send_sem=send.at[0], recv_sem=recv.at[0],
        device_id=partner, device_id_type=MESH,
    )
    across = pltpu.make_async_remote_copy(
        src_ref=buffer.at[:, c], dst_ref=buffer.at[:, c], send_sem=send.at[1], recv_sem=recv.at[1],
        device_id=partner, device_id_type=MESH,
    )

    def begin():
        @pl.loop(1, devices)
        def _(k):
            other = lax.rem(place + k, devices)
            pltpu.make_async_remote_copy(
                src_ref=buffer.at[place, c], dst_ref=buffer.at[place, c],
                send_sem=send.at[0], recv_sem=recv.at[0],
                device_id={"seq": lax.div(other, 4), "head": 2 * lax.rem(other, 4) + c},
                device_id_type=MESH,
            ).start()

    def cross():
        arrived.wait_recv()
        across.start()

    def end():
        arrived.wait_send()
        across.wait()

    return begin, cross, end


class RingGather:
    FIRST = (0, 3, 1, 2)

    def __init__(self, own, out, local, send, recv):
        seq = lax.axis_index("seq")
        self.x, self.z = lax.div(seq, 4), lax.rem(seq, 4)
        self.own, self.out, self.send, self.recv = own, out, send, recv
        self.keep = pltpu.make_async_copy(own, out.at[seq], local)

    def place(self, half, p, q):
        x, z = (p, q) if half == 0 else (q, p)
        return plus(self.x, x) * 4 + plus(self.z, z)

    def move(self, half, slot):
        if slot < 4:
            kind, block, target = slot, None, [(1, 0), (3, 0), (1, 0), (3, 0)][slot]
            origin = [(0, 0), (0, 0), (3, 0), (1, 0)][slot]
        else:
            block, kind = divmod(slot - 4, 4)
            target = [(0, 1), (0, 3), (0, 1), (0, 3)][kind]
            origin = (self.FIRST[block], [0, 0, 3, 1][kind])
        ref = self.out.at[self.place(half, *origin), half]
        if kind >= 2:
            part = ref.shape[0] // 2
            ref = ref.at[pl.ds((kind - 2) * part, part)]
        source = self.own.at[half] if origin == (0, 0) else ref
        return pltpu.make_async_remote_copy(
            src_ref=source, dst_ref=ref,
            send_sem=self.send.at[20 * half + slot], recv_sem=self.recv.at[20 * half + slot],
            device_id={"seq": self.place(half, *target)}, device_id_type=MESH,
        )

    def neighbours(self):
        return [{"seq": self.place(0, *at)} for at in ((1, 0), (3, 0), (0, 1), (0, 3))]

    def on(self, slots, *following):
        for half in range(2):
            for slot in slots:
                self.move(half, slot).wait_recv()
            for slot in following:
                self.move(half, slot).start()

    def begin(self):
        self.keep.start()
        self.on((), 0, 1)
        self.on((), 4, 5)

    def first(self):
        self.on((0,), 2, 8, 9)
        self.on((1,), 3, 12, 13)

    def second(self):
        self.on((4,), 6)
        self.on((5,), 7)
        self.on((2, 3), 16, 17)

    def third(self):
        for block in (1, 2):
            self.on((4 + 4 * block,), 6 + 4 * block)
            self.on((5 + 4 * block,), 7 + 4 * block)

    def fourth(self):
        self.on((16,), 18)
        self.on((17,), 19)

    def end(self):
        self.on((6, 7, 10, 11, 14, 15, 18, 19))
        self.keep.wait()
        for half in range(2):
            for slot in range(20):
                self.move(half, slot).wait_send()


def first_kernel(
    rows, latent_ref, turn_ref, fine_a, fine_b, gain_ref, wq_ref, wk_ref, wv_ref, win_ref, up_ref,
    kv_ref, h_ref, n_ref, eq_ref, aq_ref, akv_ref, g_ref, x_out, edge_out, full_ref,
    x_ref, edge_ref, shard, scaled_0, scaled_1, high_0, high_1, mean_0, mean_1, base, wkv, gw, wsum, edge_rows,
    loads, xsend, xrecv, local, gsend, grecv,
):
    step, steps = pl.program_id(0), pl.num_programs(0)
    seq, y, c = seat()
    width = wk_ref.shape[1]
    fetches = [
        pltpu.make_async_copy(ref, wkv.at[:, pl.ds(k * width, width)], loads.at[k])
        for k, ref in enumerate((wk_ref, wv_ref))
    ]
    begin, cross, end = spread(x_ref, xsend, xrecv)
    count = lax.axis_size("seq")
    edge = pltpu.make_async_remote_copy(
        src_ref=edge_rows, dst_ref=edge_ref, send_sem=xsend.at[2], recv_sem=xrecv.at[2],
        device_id={"seq": lax.rem(seq + count - 1, count)}, device_id_type=MESH,
    )
    ring = RingGather(shard, full_ref, local, gsend, grecv)
    fetches.append(pltpu.make_async_copy(up_ref, shard, loads.at[2]))

    def fill(block, scaled, high, mean):
        total = jnp.zeros((rows, 1), F32)
        wide = 512
        for at in range(0, HALF, wide):
            cols = slice(at, at + wide)
            sin_a, cos_a = turn_ref[block, 0:1, cols], turn_ref[block, 1:2, cols]
            sin_b, cos_b = base[0, :, cols], base[1, :, cols]
            for part, offset in (
                (sin_a * cos_b + cos_a * sin_b, 0),
                (cos_a * cos_b - sin_a * sin_b, HALF),
            ):
                into = slice(offset + at, offset + at + wide)
                high[:, into] = part.astype(BF16)
                scaled[:, into] = (part * gain_ref[:, into]).astype(BF16)
                total = total + jnp.sum(part, axis=1, keepdims=True)
        mean[...] = total * (1.0 / D)

    def tables():
        edge_rows[...] = latent_ref[0:8, :]
        own = pl.ds(pl.multiple_of((2 * y + c) * (rows // 8), rows // 8), rows // 8)
        x_ref[seq * 4 + y, c] = latent_ref[own, :].astype(BF16)

        @pl.loop(0, rows // 16)
        def _(k):
            sin_a, cos_a = fine_a[k, 0:1, :], fine_a[k, 1:2, :]
            sin_b, cos_b = fine_b[0], fine_b[1]
            into = pl.ds(pl.multiple_of(k * 16, 16), 16)
            base[0, into, :] = sin_a * cos_b + cos_a * sin_b
            base[1, into, :] = cos_a * cos_b - sin_a * sin_b

        wsum[...] = dot_t(jnp.ones((16, D), BF16), win_ref[...])
        gain = gain_ref[...]
        high = gain.astype(BF16).astype(F32)
        line = lax.broadcasted_iota(jnp.int32, (16, D), 0)
        both = jnp.where(line == 0, high, jnp.where(line == 1, gain - high, 0.0)).astype(BF16)
        for fetch in fetches:
            fetch.wait()
        gw[:, 0:width] = dot(both, wq_ref[...])
        gw[:, width:] = dot(both, wkv[...])
        gw[0:1, :] = jnp.sum(gw[...], axis=0, keepdims=True)

    @pl.when(step == 0)
    def _():
        for fetch in fetches:
            fetch.start()
        greet_all(x_ref.shape[0], tables)
        begin()
        edge.start()
        ring.begin()
        fill(0, scaled_0, high_0, mean_0)

    def work(scaled, high, mean, others):
        value = mean[...]
        kv_ref[...] = dot(scaled[...], wkv[...]) - value * gw[0:1, width:]
        h_ref[...] = dot_t(high[...], win_ref[...]) - value * wsum[0:1, :]
        n_ref[...] = HALF - D * value * value
        fill(jnp.minimum(step + 1, steps - 1), *others)

        @pl.when(step == seq)
        def _():
            eq_ref[...] = dot(scaled[...], wq_ref[...]) - value * gw[0:1, 0:width]

    even, odd = (scaled_0, high_0, mean_0), (scaled_1, high_1, mean_1)

    @pl.when(lax.rem(step, 2) == 0)
    def _():
        work(*even, odd)

    @pl.when(lax.rem(step, 2) == 1)
    def _():
        work(*odd, even)

    @pl.when(step == 3)
    def _():
        cross()

    @pl.when(step == 5)
    def _():
        ring.first()

    @pl.when(step == 11)
    def _():
        ring.second()

    @pl.when(step == steps - 1)
    def _():
        ring.third()
        wide = win_ref[...].astype(F32)
        center = wide - jnp.mean(wide, axis=1, keepdims=True)
        high, low = split_two(center * gain_ref[...])
        scaled_0[0:C, :] = high
        scaled_0[C : 2 * C, :] = low
        for into, weight in ((aq_ref, wq_ref), (akv_ref, wkv)):
            both = dot(scaled_0[0 : 2 * C, :], weight[...])
            high, low = split_two(both[:C] + both[C:])
            into[0:C, :] = high
            into[C : 2 * C, :] = low
        ring.fourth()
        high, low = split_two(center)
        high_0[0:C, :] = high
        high_1[0:C, :] = low
        high, low = high_0[0:C, :], high_1[0:C, :]
        high, low = split_two(dot_t(high, high) + dot_t(high, low) + dot_t(low, high))
        g_ref[0:C, :] = high
        g_ref[C : 2 * C, :] = low
        end()
        edge.wait()
        x_out[...] = x_ref[...]
        edge_out[...] = edge_ref[...]
        ring.end()


def ring_scratch():
    return [
        pltpu.SemaphoreType.DMA,
        pltpu.SemaphoreType.DMA((40,)),
        pltpu.SemaphoreType.DMA((40,)),
    ]


def first(rows, blocks, places, latent, gain, w_query, w_key, w_value, w_in, up):
    freq = frequencies()
    scale = jnp.array([rows, 16.0, 1.0], F32)[:, None] * jnp.arange(16, dtype=F32)[None, :]
    angles = scale[:, :, None] * freq[None, None, :]
    sines, cosines = jnp.sin(angles), jnp.cos(angles)
    turn = jnp.stack([sines[0], cosines[0]], axis=1)
    fine_a = jnp.stack([sines[1], cosines[1]], axis=1)
    fine_b = jnp.stack([sines[2], cosines[2]], axis=0)
    return first_call(rows, blocks, places, latent, turn, fine_a, fine_b, gain, w_query, w_key,
                      w_value, w_in, up)


def first_call(rows, blocks, places, latent, turn, fine_a, fine_b, gain, w_query, w_key, w_value,
               w_in, up):
    width = w_key.shape[1]
    length = rows * blocks
    whole = pl.BlockSpec(memory_space=pltpu.VMEM)
    far = pl.BlockSpec(memory_space=pl.ANY)
    return pl.pallas_call(
        functools.partial(first_kernel, rows),
        grid=(blocks,),
        in_specs=[whole] * 6 + [far, far, whole, far],
        out_specs=[
            pl.BlockSpec((rows, 2 * width), lambda i: (i, 0)),
            pl.BlockSpec((rows, C), lambda i: (i, 0)),
            pl.BlockSpec((rows, 1), lambda i: (i, 0)),
        ]
        + [whole] * 6
        + [far],
        out_shape=[
            jax.ShapeDtypeStruct((length, 2 * width), F32),
            jax.ShapeDtypeStruct((length, C), F32),
            jax.ShapeDtypeStruct((length, 1), F32),
            jax.ShapeDtypeStruct((rows, width), F32),
            jax.ShapeDtypeStruct((2 * C, width), BF16),
            jax.ShapeDtypeStruct((2 * C, 2 * width), BF16),
            jax.ShapeDtypeStruct((2 * C, C), BF16),
            jax.ShapeDtypeStruct((places, 2, rows // 8, C), BF16),
            jax.ShapeDtypeStruct((8, C), F32),
            jax.ShapeDtypeStruct((blocks, *up.shape), BF16),
        ],
        scratch_shapes=[
            pltpu.VMEM((places, 2, rows // 8, C), BF16),
            pltpu.VMEM((8, C), F32),
            pltpu.VMEM(up.shape, BF16),
        ]
        + [pltpu.VMEM((rows, D), BF16)] * 4
        + [pltpu.VMEM((rows, 1), F32)] * 2
        + [
            pltpu.VMEM((2, rows, HALF), F32),
            pltpu.VMEM((D, 2 * width), BF16),
            pltpu.VMEM((16, 3 * width), F32),
            pltpu.VMEM((16, C), F32),
            pltpu.VMEM((8, C), F32),
            pltpu.SemaphoreType.DMA((3,)),
            pltpu.SemaphoreType.DMA((3,)),
            pltpu.SemaphoreType.DMA((3,)),
        ]
        + ring_scratch(),
        compiler_params=pltpu.CompilerParams(
            collective_id=0, has_side_effects=True, vmem_limit_bytes=44 << 20
        ),
        cost_estimate=pl.CostEstimate(
            flops=60_000_000_000, bytes_accessed=40_000_000, transcendentals=0
        ),
        name="first",
    )(latent, turn, fine_a, fine_b, gain, w_query, w_key, w_value, w_in, up)


def reduce_over_head(produce, meanwhile, term, taken, via_out, via_in, near, fin, send, recv):
    _, y, c = seat()
    partner, up, down = 2 * y + 1 - c, 2 * plus(y, 1) + c, 2 * plus(y, 3) + c

    def copy(src, dst, slot, head):
        return pltpu.make_async_remote_copy(
            src_ref=src, dst_ref=dst, send_sem=send.at[slot], recv_sem=recv.at[slot],
            device_id={"head": head}, device_id_type=MESH,
        )

    def pair(half, at):
        return term[half, at, c].astype(F32) + taken[half, at].astype(F32)

    gives = []
    for half in range(2):
        produce(half)
        gives.append(copy(term.at[half, :, 1 - c], taken.at[half], half, partner))
        gives[half].start()
    meanwhile()
    across, ahead, behind = plus(y, 2), plus(y, 1), plus(y, 3)
    gives[0].wait_recv()
    via_out[0] = pair(0, across).astype(BF16)
    via_0 = copy(via_out.at[0], via_in.at[0], 2, up)
    via_0.start()
    near[1, 0] = pair(0, behind).astype(BF16)
    down_0 = copy(near.at[1, 0], fin.at[1, 0], 6, down)
    down_0.start()
    gives[1].wait_recv()
    via_out[1] = pair(1, across).astype(BF16)
    via_1 = copy(via_out.at[1], via_in.at[1], 3, down)
    via_1.start()
    near[0, 1] = pair(1, ahead).astype(BF16)
    up_1 = copy(near.at[0, 1], fin.at[0, 1], 5, up)
    up_1.start()
    via_0.wait_recv()
    near[0, 0] = (pair(0, ahead) + via_in[0].astype(F32)).astype(BF16)
    up_0 = copy(near.at[0, 0], fin.at[0, 0], 4, up)
    up_0.start()
    via_1.wait_recv()
    near[1, 1] = (pair(1, behind) + via_in[1].astype(F32)).astype(BF16)
    down_1 = copy(near.at[1, 1], fin.at[1, 1], 7, down)
    down_1.start()
    sums = [pair(half, y) for half in range(2)]
    down_0.wait_recv()
    up_0.wait_recv()
    first = sums[0] + fin[0, 0].astype(F32) + fin[1, 0].astype(F32)
    up_1.wait_recv()
    down_1.wait_recv()
    second = sums[1] + fin[0, 1].astype(F32) + fin[1, 1].astype(F32)
    for done in (*gives, via_0, via_1, up_0, up_1, down_0, down_1):
        done.wait_send()
    return jnp.concatenate([first, second], axis=1)


def gather_over_head(out, send, recv, midway=lambda: None):
    _, y, c = seat()
    partner, up, down = 2 * y + 1 - c, 2 * plus(y, 1) + c, 2 * plus(y, 3) + c
    across, ahead, behind = plus(y, 2), plus(y, 1), plus(y, 3)
    low, high = pl.ds(0, HALF), pl.ds(HALF, HALF)

    def copy(block, slot, head):
        return pltpu.make_async_remote_copy(
            src_ref=block, dst_ref=block, send_sem=send.at[slot], recv_sem=recv.at[slot],
            device_id={"head": head}, device_id_type=MESH,
        )

    moves = [copy(out.at[y, c], 0, up), copy(out.at[y, c], 1, down), copy(out.at[y, c], 2, partner)]
    for move in moves:
        move.start()

    def then(slot, *following):
        moves[slot].wait_recv()
        for move in following:
            move.start()
            moves.append(move)

    then(0, copy(out.at[behind, c, :, low], 3, up), copy(out.at[behind, c], 4, partner))
    then(1, copy(out.at[ahead, c, :, high], 5, down), copy(out.at[ahead, c], 6, partner))
    midway()
    then(3, copy(out.at[across, c, :, low], 7, partner))
    then(5, copy(out.at[across, c, :, high], 8, partner))
    for slot in (2, 4, 6, 7, 8):
        moves[slot].wait_recv()
    for move in moves:
        move.wait_send()


def reduce_scratch(share):
    return [
        pltpu.VMEM((2, 4, 2, share, HALF), BF16),
        pltpu.VMEM((2, 4, share, HALF), BF16),
        pltpu.VMEM((2, share, HALF), BF16),
        pltpu.VMEM((2, share, HALF), BF16),
        pltpu.VMEM((2, 2, share, HALF), BF16),
        pltpu.VMEM((2, 2, share, HALF), BF16),
        pltpu.SemaphoreType.DMA((8,)),
        pltpu.SemaphoreType.DMA((8,)),
    ]


def head_neighbours():
    _, y, c = seat()
    return [{"head": 2 * y + 1 - c}, {"head": 2 * plus(y, 1) + c}, {"head": 2 * plus(y, 3) + c}]


def store_terms(term, half, at, share, value):
    for block in range(8):
        rows = value[block * share : (block + 1) * share].astype(BF16)
        term[half, block // 2, block % 2, :, at : at + value.shape[1]] = rows


def block_kernel(rows, heads, ringed, *refs):
    (
        x_ref, kv_ref, h_ref, n_ref, eq_ref, aq_ref, akv_ref, g_ref,
        embedding_ref, win_ref, wo_ref, gain_ref, *refs,
    ) = refs
    if ringed:
        shard_ref, stream_ref, normed_out, full_ref, *refs = refs
        *refs, shard, load, local, gsend, grecv = refs
        ring = RingGather(shard, full_ref, local, gsend, grecv)
        fetch = pltpu.make_async_copy(shard_ref, shard, load)
    else:
        stream_ref, normed_out, *refs = refs
    normed_ref, queries, acc, sums, attended, *parts, send, recv = refs
    term = parts[0]
    share = rows // 8
    width = heads * HEAD_DIM
    block = pl.program_id(0)
    me, y, c = seat()

    def scale_of(x, h, n):
        twice = jnp.concatenate([x, x], axis=1)
        quad = jnp.sum(x.astype(F32) * (dot(twice, g_ref[...]) + 2.0 * h), axis=1, keepdims=True)
        return twice, lax.rsqrt(jnp.maximum(quad + n, 0.0) * (1.0 / D) + EPSILON)

    @pl.when(block == 0)
    def _():
        if ringed:
            fetch.start()
        greet(head_neighbours() + (ring.neighbours() if ringed else []))
        if ringed:
            fetch.wait()
            ring.begin()
        own = pl.ds(pl.multiple_of(me * rows, rows), rows)
        twice, scale = scale_of(x_ref[own, :], h_ref[own, :], n_ref[own, :])
        value = (dot(twice, aq_ref[...]) + eq_ref[...]) * (scale * HEAD_DIM**-0.5)
        queries[...] = value.astype(BF16)
        acc[...] = jnp.zeros_like(acc)
        sums[...] = jnp.zeros_like(sums)

    def step(masked):
        here = pl.ds(pl.multiple_of(block * KEY_BLOCK, KEY_BLOCK), KEY_BLOCK)
        twice, scale = scale_of(x_ref[here, :], h_ref[here, :], n_ref[here, :])
        both = ((dot(twice, akv_ref[...]) + kv_ref[...]) * scale).astype(BF16)
        keys, values = both[:, :width], both[:, width:]
        if masked:
            shape = (rows, KEY_BLOCK)
            row = me * rows + lax.broadcasted_iota(jnp.int32, shape, 0)
            col = block * KEY_BLOCK + lax.broadcasted_iota(jnp.int32, shape, 1)
            seen = col <= row
        for head in range(heads):
            cols = slice(head * HEAD_DIM, (head + 1) * HEAD_DIM)
            scores = dot_t(queries[:, cols], keys[:, cols])
            if masked:
                weights = jnp.where(seen, jnp.exp(jnp.where(seen, scores, 0.0)), 0.0)
            else:
                weights = jnp.exp(scores)
            part = weights[:, :HEAD_DIM]
            for at in range(HEAD_DIM, KEY_BLOCK, HEAD_DIM):
                part = part + weights[:, at : at + HEAD_DIM]
            sums[:, cols] += part
            acc[:, cols] += dot(weights.astype(BF16), values[:, cols])

    final = (me * rows + rows - 1) // KEY_BLOCK

    @pl.when(block < final)
    def _():
        step(False)

    @pl.when(block == final)
    def _():
        step(True)

    def produce(half):
        for at in range(0, HALF, 768):
            cols = slice(half * HALF + at, half * HALF + at + 768)
            store_terms(term, half, at, share, dot(attended[...], wo_ref[:, cols]))

    def meanwhile():
        first = pl.ds(pl.multiple_of(me * rows + (2 * y + c) * share, share), share)
        stream_ref[...] = dot(x_ref[first, :], win_ref[...]) + embedding_ref[...]
        if ringed:
            ring.first()

    @pl.when(block == pl.num_programs(0) - 1)
    def _():
        for head in range(heads):
            cols = slice(head * HEAD_DIM, (head + 1) * HEAD_DIM)
            total = jnp.sum(sums[:, cols], axis=1, keepdims=True)
            attended[:, cols] = (acc[:, cols] / total).astype(BF16)
        total = reduce_over_head(produce, meanwhile, *parts)
        stream = stream_ref[...] + total
        stream_ref[...] = stream
        normed_ref[y, c] = layer_norm(stream, gain_ref[...]).astype(BF16)
        gather_over_head(normed_ref, send, recv, ring.second if ringed else lambda: None)
        normed_out[...] = normed_ref[...]
        if ringed:
            ring.third()
            ring.fourth()
            ring.end()


def block_step(rows, state, x, embedding, w_in, w_attn_out, gain, shard=None):
    kv = state[0]
    length, width = kv.shape[0], kv.shape[1] // 2
    share = rows // 8
    ringed = shard is not None
    whole = pl.BlockSpec(memory_space=pltpu.VMEM)
    far = pl.BlockSpec(memory_space=pl.ANY)
    tile = pl.BlockSpec((KEY_BLOCK, 2 * width), lambda i: (i, 0))
    more = [shard] if ringed else []
    outs = [
        jax.ShapeDtypeStruct((share, D), F32),
        jax.ShapeDtypeStruct((4, 2, share, D), BF16),
    ]
    if ringed:
        outs.append(jax.ShapeDtypeStruct((length // rows, *shard.shape), BF16))
    return pl.pallas_call(
        functools.partial(block_kernel, rows, width // HEAD_DIM, ringed),
        grid=(length // KEY_BLOCK,),
        in_specs=[whole, tile] + [whole] * 10 + [far] * ringed,
        out_specs=[whole] * 2 + [far] * ringed,
        out_shape=outs,
        scratch_shapes=[
            pltpu.VMEM((4, 2, share, D), BF16),
            pltpu.VMEM((rows, width), BF16),
            pltpu.VMEM((rows, width), F32),
            pltpu.VMEM((rows, width), F32),
            pltpu.VMEM((rows, width), BF16),
        ]
        + reduce_scratch(share)
        + [pltpu.SemaphoreType.DMA((9,)), pltpu.SemaphoreType.DMA((9,))]
        + ([pltpu.VMEM(shard.shape, BF16), pltpu.SemaphoreType.DMA] + ring_scratch() if ringed else []),
        compiler_params=pltpu.CompilerParams(
            collective_id=1 if ringed else 4, has_side_effects=True, vmem_limit_bytes=40 << 20
        ),
        cost_estimate=pl.CostEstimate(
            flops=30_000_000_000, bytes_accessed=20_000_000, transcendentals=0
        ),
        name="block_ring" if ringed else "block",
    )(x, *state, embedding, w_in, w_attn_out, gain, *more)


def mlp_kernel(
    share, last, normed_ref, up_ref, down_ref, stream_ref, gain_ref, wf_ref, ahead_ref, out_ref,
    up, down, hidden, loads, *scratch,
):
    *parts, send, recv = scratch
    term = parts[0]
    seq, y, c = seat()
    ups, downs = up.shape[0], down.shape[0]
    wide, tall = up.shape[2], down.shape[1]
    fetches = [
        pltpu.make_async_copy(up_ref.at[:, pl.ds(k * wide, wide)], up.at[k], loads.at[k])
        for k in range(ups)
    ] + [
        pltpu.make_async_copy(
            down_ref.at[pl.ds(k * tall, tall), :], down.at[k], loads.at[ups + k]
        )
        for k in range(downs)
    ]
    for fetch in fetches:
        fetch.start()
    if last:
        mirror = lax.axis_size("seq") - 1 - seq
        sends_edge = jnp.logical_and(mirror > 0, 2 * y + c == 7)
        keeps_edge = jnp.logical_and(mirror - 1 == seq, 2 * y + c == 7)
        waits_edge = jnp.logical_and(mirror > 0, jnp.logical_not(keeps_edge))
        barrier = pltpu.get_barrier_semaphore()
        for target in head_neighbours():
            pl.semaphore_signal(barrier, inc=1, device_id=target, device_id_type=MESH)
        for head in range(8):
            pl.semaphore_signal(
                barrier, inc=1, device_id={"seq": mirror, "head": head}, device_id_type=MESH
            )

        @pl.when(waits_edge)
        def _():
            pl.semaphore_signal(
                barrier, inc=1, device_id={"seq": mirror - 1, "head": 7}, device_id_type=MESH
            )

        @pl.when(keeps_edge)
        def _():
            pl.semaphore_wait(barrier, 18)

        @pl.when(jnp.logical_and(sends_edge, jnp.logical_not(keeps_edge)))
        def _():
            pl.semaphore_wait(barrier, 19)

        @pl.when(jnp.logical_not(sends_edge))
        def _():
            pl.semaphore_wait(barrier, 11)

    else:
        greet_all(out_ref.shape[0])

    for k in range(ups):
        fetches[k].wait()
        pre = dot(normed_ref[...], up[k])
        hidden[:, k * wide : (k + 1) * wide] = jax.nn.gelu(pre, approximate=True).astype(BF16)

    def produce(half):
        for at in range(downs // 2):
            k = half * (downs // 2) + at
            fetches[ups + k].wait()
            store_terms(term, half, at * tall, share, dot_t(hidden[...], down[k]))

    total = reduce_over_head(produce, lambda: None, *parts)
    normed = layer_norm(stream_ref[...] + total, gain_ref[...]).astype(BF16)
    params = dot(normed, wf_ref[...])
    following = ahead_ref[...] * jnp.exp(jnp.tanh(params[:, C:])) + params[:, :C]
    if not last:
        out_ref[seq * 4 + y, c] = following.astype(BF16)
        begin, cross, end = spread(out_ref, send, recv)
        begin()
        cross()
        end()
    else:
        block = scratch[0].at[0, 0, 0, :, pl.ds(0, C)]
        block[...] = following.astype(BF16)
        head = 2 * y + c
        moves = [
            pltpu.make_async_remote_copy(
                src_ref=block, dst_ref=out_ref.at[head], send_sem=send.at[k], recv_sem=recv.at[0],
                device_id={"seq": mirror, "head": k}, device_id_type=MESH,
            )
            for k in range(8)
        ]
        edges = [
            pltpu.make_async_remote_copy(
                src_ref=block, dst_ref=out_ref.at[8], send_sem=send.at[8 + k], recv_sem=recv.at[1],
                device_id={"seq": mirror - 1, "head": k}, device_id_type=MESH,
            )
            for k in range(8)
        ]
        for move in moves:
            move.start()

        @pl.when(sends_edge)
        def _():
            for move in edges[:7]:
                move.start()

        @pl.when(jnp.logical_and(sends_edge, jnp.logical_not(keeps_edge)))
        def _():
            edges[7].start()

        whole = out_ref.at[pl.ds(0, 8)]
        pltpu.make_async_remote_copy(
            src_ref=whole, dst_ref=whole, send_sem=send.at[0], recv_sem=recv.at[0],
            device_id={"seq": mirror, "head": 0}, device_id_type=MESH,
        ).wait_recv()

        @pl.when(waits_edge)
        def _():
            pltpu.make_async_remote_copy(
                src_ref=block, dst_ref=out_ref.at[8], send_sem=send.at[0], recv_sem=recv.at[1],
                device_id={"seq": mirror - 1, "head": 7}, device_id_type=MESH,
            ).wait_recv()

        for move in moves:
            move.wait_send()

        @pl.when(sends_edge)
        def _():
            for move in edges[:7]:
                move.wait_send()

        @pl.when(jnp.logical_and(sends_edge, jnp.logical_not(keeps_edge)))
        def _():
            edges[7].wait_send()

        @pl.when(jnp.logical_not(waits_edge))
        def _():
            out_ref[8] = following.astype(BF16)


def mlp(share, places, last, normed, up, down, stream, gain, w_final, ahead):
    whole = pl.BlockSpec(memory_space=pltpu.VMEM)
    rows, width = normed.shape[0], up.shape[1]
    shape = (9, share, C) if last else (places, 2, share, C)
    return pl.pallas_call(
        functools.partial(mlp_kernel, share, last),
        in_specs=[whole] + [pl.BlockSpec(memory_space=pl.ANY)] * 2 + [whole] * 4,
        out_specs=whole,
        out_shape=jax.ShapeDtypeStruct(shape, BF16),
        scratch_shapes=[
            pltpu.VMEM((3, D, width // 3), BF16),
            pltpu.VMEM((4, D // 4, width), BF16),
            pltpu.VMEM((rows, width), BF16),
            pltpu.SemaphoreType.DMA((7,)),
        ]
        + reduce_scratch(share)
        + [pltpu.SemaphoreType.DMA((16,)), pltpu.SemaphoreType.DMA((2,))],
        compiler_params=pltpu.CompilerParams(
            collective_id=3 if last else 2, has_side_effects=True, vmem_limit_bytes=44 << 20
        ),
        cost_estimate=pl.CostEstimate(
            flops=40_000_000_000, bytes_accessed=30_000_000, transcendentals=0
        ),
        name="mlp_last" if last else "mlp",
    )(normed, up, down, stream, gain, w_final, ahead)


def per_device(
    latent, w_in, w_query, w_key, w_value, w_attn_out, w_up, w_down, w_final,
    gain_attn, gain_mlp, gain_final,
):
    seq_count, head_count = lax.axis_size("seq"), lax.axis_size("head")
    me, mine = lax.axis_index("seq"), lax.axis_index("head")
    rows = latent.shape[0]
    share = rows // head_count
    length = rows * seq_count
    places = seq_count * head_count // 2
    start = me * rows + mine * share

    shape = (2, w_up.shape[0] // 2, w_up.shape[1])
    *state, gathered, edge, up = first(
        rows, seq_count, places, latent, gain_attn[None, :], w_query, w_key, w_value, w_in,
        w_up.reshape(shape),
    )
    up = up.reshape(D, w_up.shape[1])
    x = gathered.reshape(length, C)
    angles = (start + jnp.arange(share)).astype(F32)[:, None] * frequencies()[None, :]
    embedding = jnp.concatenate([jnp.sin(angles), jnp.cos(angles)], axis=1)
    ahead = lax.dynamic_slice_in_dim(
        jnp.concatenate([latent[1:], edge[:1]], axis=0), mine * share, share, 0
    )
    top = x[:1]
    for step_index in range(ITERS):
        last = step_index == ITERS - 1
        stream, normed, *full = block_step(
            rows, state, x, embedding, w_in, w_attn_out, gain_mlp[None, :],
            w_down.T.reshape(shape) if step_index == 0 else None,
        )
        if step_index == 0:
            down = full[0].reshape(D, w_up.shape[1])
        following = mlp(
            share, places, last, normed.reshape(rows, D), up, down, stream, gain_final[None, :],
            w_final, ahead,
        )
        if not last:
            x = jnp.concatenate([top, following.reshape(length, C)[:-1]], axis=0)
    edge = jnp.where(me == seq_count - 1, top, following[8, share - 1 :])
    result = jnp.concatenate([edge, following[:8].reshape(rows, C)[:-1]], axis=0)
    return result[::-1].astype(F32)


def solution(mesh):
    in_specs = (
        P("seq", None),
        P(),
        P(None, "head"),
        P(None, "head"),
        P(None, "head"),
        P("head", None),
        P("seq", "head"),
        P("head", "seq"),
        P(),
        P(),
        P(),
        P(),
    )
    return jax.shard_map(
        per_device, mesh=mesh, in_specs=in_specs, out_specs=P("seq", None), check_vma=False
    )
```

profile of v0, /device:TPU:1, one launch (start us, length us, event | category | flops | bytes accessed | tf_op | source)
XLA Modules:
  0.0 255.8 jit_solution(595499872176285244)
XLA Ops:
  0.0 0.0 copy-start.9
  0.0 0.0 copy-start.7
  0.0 0.0 copy-start
  0.0 0.0 copy-start.4
  0.0 0.8 iota_multiply_fusion
  0.9 1.1 multiply_sine_fusion
  2.1 0.2 copy.15.fine_a
  2.3 0.2 copy.14.turn_ref
  2.4 0.0 copy-done.9
  2.4 0.0 copy-done.7
  2.4 0.0 copy-done
  2.5 0.0 copy-done.4
  2.5 0.0 copy-start.10
  2.5 70.8 %first.1 = (f32[4096,768]{1,0:T(8,128)}, f32[4096,128]{1,0:T(8,128)S(1)}, f32[4096,1]{1,0:T(8,128)S(1)}, f32[256,384]{1,0:T(8,128)S(1)}, bf16[256,384]{1,0:T(8,1...) custom-call(f32[256,128]{1,0:T(8,128)S(1)} %copy-done, ...), custom_call_target="tpu_custom_call" | custom-call | flops 60000002048 | bytes 40000000 | tf_op jit(solution)/shard_map/first/pallas_call | solution.py:352
  73.2 0.0 copy-start.14
  73.3 1.3 copy-done.14
  74.6 0.0 copy-start.17
  74.6 1.3 copy-done.17
  75.9 0.0 copy-start.20
  75.9 0.8 copy-done.20
  76.6 0.0 copy-start.23
  76.6 0.8 copy-done.23
  77.4 0.8 multiply_sine_fusion.1
  78.2 0.0 copy-done.10
  78.2 0.0 copy-start.1
  78.2 1.7 copy-done.1
  79.9 0.0 copy-start.5
  79.9 1.1 copy-done.5
  81.0 0.0 copy-start.8
  81.0 1.1 copy-done.8
  82.1 0.0 copy-start.15
  82.1 1.6 copy-done.15
  83.7 0.0 copy-start.18
  83.7 1.6 copy-done.18
  85.2 0.0 copy-start.21
  85.2 1.0 copy-done.21
  86.2 0.0 copy-start.24
  86.2 1.0 copy-done.24
  87.2 0.0 copy-start.3
  87.2 0.0 copy-start.11
  87.2 56.5 %block_ring.1 = (f32[32,3072]{1,0:T(8,128)S(1)}, bf16[4,2,32,3072]{3,2,1,0:T(8,128)(2,1)S(1)}, bf16[16,2,96,1536]{3,2,1,0:T(8,128)(2,1)}) custom-call(bf16[4096,128]{1,0:T(8,128)(2,1)S(1)} %bitcast.27, f32[4096,768]{1,0:T(8,128)} %get-tuple-element.21.refs_1_, f32[4096,128]{1,0:T(8,128)S(1)} %copy-done.15, f32[4096,1]{1,0:T(8,128)S(1)} %copy-done.18, ...), custom_call_target="tpu_custom_call" | custom-call | flops 30000001024 | bytes 20000000 | tf_op jit(solution)/shard_map/block_ring/pallas_call | solution.py:630
  143.8 0.0 copy-start.12
  143.8 1.2 copy-done.12
  144.9 0.8 copy-done.26
  145.8 0.0 copy-done.3
  145.8 0.0 copy-done.11
  145.8 0.0 copy-start.13
  145.8 1.4 copy-done.13
  147.2 1.0 copy-done.27
  148.2 37.4 %mlp.1 = bf16[64,2,32,128]{3,2,1,0:T(8,128)(2,1)S(1)} custom-call(bf16[256,3072]{1,0:T(8,128)(2,1)S(1)} %bitcast.37, bf16[3072,1536]{1,0:T(8,128)(2,1)} %bitcast.40, bf16[3072,1536]{1,0:T(8,128)(2,1)} %bitcast.42, f32[32,3072]{1,0:T(8,128)S(1)} %copy-done.27, f32[1,3072]{1,0:T(1,128)S(1)} %bitcast.35, bf16[3072,256]{1,0:T(8,128)(2,1)S(1)} %copy-done.3, ...), custom_call_target="tpu_custom_call" | custom-call | flops 40000000000 | bytes 30000000 | tf_op jit(solution)/shard_map/mlp/pallas_call | solution.py:795
  185.6 0.0 copy-start.6
  185.6 0.0 copy-start.22
  185.7 0.0 copy-start.25
  185.7 0.3 pad_maximum_fusion.refs_0_
  186.0 0.0 copy-done.2
  186.0 0.0 copy-done.16
  186.0 0.0 copy-done.19
  186.0 0.8 copy-done.6
  186.8 0.1 copy-done.22
  186.9 0.1 copy-done.25
  187.0 34.4 %block.1 = (f32[32,3072]{1,0:T(8,128)S(1)}, bf16[4,2,32,3072]{3,2,1,0:T(8,128)(2,1)S(1)}) custom-call(bf16[4096,128]{1,0:T(8,128)(2,1)S(1)} %pad_maximum_fusion.refs_0_, f32[4096,768]{1,0:T(8,128)} %get-tuple-element.21.refs_1_, f32[4096,128]{1,0:T(8,128)S(1)} %copy-done.16, f32[4096,1]{1,0:T(8,128)S(1)} %copy-done.19, f32[256,384]{1,0:T(8,128)S(1)} %copy-done.22, ...), custom_call_target="tpu_custom_call" | custom-call | flops 30000001024 | bytes 20000000 | tf_op jit(solution)/shard_map/block/pallas_call | solution.py:630
  221.4 33.5 %mlp_last.1 = bf16[9,32,128]{2,1,0:T(8,128)(2,1)S(1)} custom-call(bf16[256,3072]{1,0:T(8,128)(2,1)S(1)} %bitcast.38, bf16[3072,1536]{1,0:T(8,128)(2,1)} %bitcast.41, bf16[3072,1536]{1,0:T(8,128)(2,1)} %bitcast.43, f32[32,3072]{1,0:T(8,128)S(1)} %get-tuple-element.34.stream_ref, f32[1,3072]{1,0:T(1,128)S(1)} %bitcast.36, bf16[3072,256]{1,0:T(8,128)(2,1)S(1)} %copy-done.3, ...), custom_call_target="tpu_custom_call" | custom-call | flops 40000000000 | bytes 30000000 | tf_op jit(solution)/shard_map/mlp_last/pallas_call | solution.py:795
  255.0 0.1 rev.3
  255.1 0.7 convert_element_type.26
  (19 shorter events, 0.2 us)
Async XLA Ops:
  0.0 2.4 copy-start.9
  0.0 2.4 copy-start.7
  0.0 2.4 copy-start
  0.0 2.4 copy-start.4
  2.5 75.7 %copy-start.10 = (f32[3072]{0:T(1024)S(1)}, f32[3072]{0:T(1024)}, u32[]{:S(2)}) copy-start(f32[3072]{0:T(1024)} %param.23) | copy-start | bytes 36868
  73.2 1.3 copy-start.14
  74.6 1.3 copy-start.17
  75.9 0.8 copy-start.20
  76.6 0.8 copy-start.23
  78.2 1.7 copy-start.1
  79.9 1.1 copy-start.5
  81.0 1.1 copy-start.8
  82.1 1.6 copy-start.15
  83.7 1.6 copy-start.18
  85.2 1.0 copy-start.21
  86.2 1.0 copy-start.24
  87.2 58.5 %copy-start.3 = (bf16[3072,256]{1,0:T(8,128)(2,1)S(1)}, bf16[3072,256]{1,0:T(8,128)(2,1)}, u32[]{:S(2)}) copy-start(bf16[3072,256]{1,0:T(8,128)(2,1)} %wf_ref.3) | copy-start | bytes 4718596
  87.2 58.5 %copy-start.11 = (f32[3072]{0:T(1024)S(1)}, f32[3072]{0:T(1024)}, u32[]{:S(2)}) copy-start(f32[3072]{0:T(1024)} %param.24) | copy-start | bytes 36868
  143.8 1.2 copy-start.12
  144.9 0.8 copy-start.26
  145.8 1.4 copy-start.13
  147.2 1.0 copy-start.27
  148.2 37.8 %copy-start.2 = (bf16[384,3072]{1,0:T(8,128)(2,1)S(1)}, bf16[384,3072]{1,0:T(8,128)(2,1)}, u32[]{:S(2)}) copy-start(bf16[384,3072]{1,0:T(8,128)(2,1)} %refs_10_.3) | copy-start | bytes 7077892
  148.2 37.8 %copy-start.16 = (f32[4096,128]{1,0:T(8,128)S(1)}, f32[4096,128]{1,0:T(8,128)}, u32[]{:S(2)}) copy-start(f32[4096,128]{1,0:T(8,128)} %copy-done.14) | copy-start | bytes 6291460
  148.2 37.8 %copy-start.19 = (f32[4096,1]{1,0:T(8,128)S(1)}, f32[4096,1]{1,0:T(8,128)}, u32[]{:S(2)}) copy-start(f32[4096,1]{1,0:T(8,128)} %copy-done.17) | copy-start | bytes 49156
  185.6 1.1 copy-start.6
  185.6 1.2 copy-start.22
  185.7 1.3 copy-start.25
where the time goes:
time: 256 us
  Pallas kernels  233 us (91%)
  local copies, waits for them, and re-layouts  19 us (7%)
  other arithmetic  3.79 us (1%)
    pallas_call x2, Pallas kernels, block_step(): pl.pallas_call(functools.partial(block_kernel, rows, width // HEAD_DIM, r...  90.9 us
    pallas_call x2, Pallas kernels, mlp(): pl.pallas_call(functools.partial(mlp_kernel, share, last), in_specs=[whol...  70.9 us
    pallas_call x1, Pallas kernels, first_call(): pl.pallas_call(functools.partial(first_kernel, rows), grid=(blocks,), in_...  70.8 us
    unnamed x56, local copies, waits for them, and re-layouts  18.5 us

commit v1 on v0

--- a/solution.py
+++ b/solution.py
@@ -44,6 +44,19 @@
 MESH = pl.DeviceIdType.MESH
 
 
+def staged(pairs, sems):
+    return [pltpu.make_async_copy(src, dst, sems.at[k]) for k, (src, dst) in enumerate(pairs)]
+
+
+def each(action, copies):
+    for copy in copies:
+        getattr(copy, action)()
+
+
+def buffer_like(array):
+    return pltpu.VMEM(array.shape, array.dtype)
+
+
 def seat():
     head = lax.axis_index("head")
     return lax.axis_index("seq"), lax.div(head, 2), lax.rem(head, 2)
@@ -53,11 +66,14 @@
     return lax.rem(y + by, 4)
 
 
-def greet(targets):
+def hail(targets):
     barrier = pltpu.get_barrier_semaphore()
     for target in targets:
         pl.semaphore_signal(barrier, inc=1, device_id=target, device_id_type=MESH)
-    pl.semaphore_wait(barrier, len(targets))
+
+
+def met(targets):
+    pl.semaphore_wait(pltpu.get_barrier_semaphore(), len(targets))
 
 
 def greet_all(devices, meanwhile=lambda: None):
@@ -170,16 +186,13 @@
     def second(self):
         self.on((4,), 6)
         self.on((5,), 7)
+
+    def middle(self):
         self.on((2, 3), 16, 17)
 
-    def third(self):
-        for block in (1, 2):
-            self.on((4 + 4 * block,), 6 + 4 * block)
-            self.on((5 + 4 * block,), 7 + 4 * block)
-
-    def fourth(self):
-        self.on((16,), 18)
-        self.on((17,), 19)
+    def third(self, block):
+        self.on((4 + 4 * block,), 6 + 4 * block)
+        self.on((5 + 4 * block,), 7 + 4 * block)
 
     def end(self):
         self.on((6, 7, 10, 11, 14, 15, 18, 19))
@@ -191,8 +204,8 @@
 
 def first_kernel(
     rows, latent_ref, turn_ref, fine_a, fine_b, gain_ref, wq_ref, wk_ref, wv_ref, win_ref, up_ref,
-    kv_ref, h_ref, n_ref, eq_ref, aq_ref, akv_ref, g_ref, x_out, edge_out, full_ref,
-    x_ref, edge_ref, shard, scaled_0, scaled_1, high_0, high_1, mean_0, mean_1, base, wkv, gw, wsum, edge_rows,
+    kv_ref, h_ref, n_ref, eq_out, aq_out, akv_out, g_out, x_out, edge_out, full_ref,
+    eq_ref, aq_ref, akv_ref, g_ref, x_ref, edge_ref, stores, shard, scaled_0, scaled_1, high_0, high_1, mean_0, mean_1, base, wkv, gw, wsum, edge_rows,
     loads, xsend, xrecv, local, gsend, grecv,
 ):
     step, steps = pl.program_id(0), pl.num_programs(0)
@@ -210,6 +223,13 @@
     )
     ring = RingGather(shard, full_ref, local, gsend, grecv)
     fetches.append(pltpu.make_async_copy(up_ref, shard, loads.at[2]))
+    results = staged(
+        [
+            (eq_ref, eq_out), (aq_ref, aq_out), (akv_ref, akv_out), (g_ref, g_out),
+            (x_ref, x_out), (edge_ref, edge_out),
+        ],
+        stores,
+    )
 
     def fill(block, scaled, high, mean):
         total = jnp.zeros((rows, 1), F32)
@@ -287,17 +307,13 @@
     def _():
         cross()
 
-    @pl.when(step == 5)
-    def _():
-        ring.first()
-
-    @pl.when(step == 11)
-    def _():
-        ring.second()
+    for at, event in ((4, ring.first), (7, ring.second), (8, ring.middle)):
+        pl.when(step == at)(event)
+    for at, block in ((11, 1), (14, 2)):
+        pl.when(step == at)(functools.partial(ring.third, block))
 
     @pl.when(step == steps - 1)
     def _():
-        ring.third()
         wide = win_ref[...].astype(F32)
         center = wide - jnp.mean(wide, axis=1, keepdims=True)
         high, low = split_two(center * gain_ref[...])
@@ -308,7 +324,7 @@
             high, low = split_two(both[:C] + both[C:])
             into[0:C, :] = high
             into[C : 2 * C, :] = low
-        ring.fourth()
+        ring.third(3)
         high, low = split_two(center)
         high_0[0:C, :] = high
         high_1[0:C, :] = low
@@ -318,9 +334,9 @@
         g_ref[C : 2 * C, :] = low
         end()
         edge.wait()
-        x_out[...] = x_ref[...]
-        edge_out[...] = edge_ref[...]
+        each("start", results)
         ring.end()
+        each("wait", results)
 
 
 def ring_scratch():
@@ -348,7 +364,7 @@
     width = w_key.shape[1]
     length = rows * blocks
     whole = pl.BlockSpec(memory_space=pltpu.VMEM)
-    far = pl.BlockSpec(memory_space=pl.ANY)
+    far = pl.BlockSpec(memory_space=pltpu.HBM)
     return pl.pallas_call(
         functools.partial(first_kernel, rows),
         grid=(blocks,),
@@ -358,8 +374,7 @@
             pl.BlockSpec((rows, C), lambda i: (i, 0)),
             pl.BlockSpec((rows, 1), lambda i: (i, 0)),
         ]
-        + [whole] * 6
-        + [far],
+        + [far] * 7,
         out_shape=[
             jax.ShapeDtypeStruct((length, 2 * width), F32),
             jax.ShapeDtypeStruct((length, C), F32),
@@ -373,8 +388,13 @@
             jax.ShapeDtypeStruct((blocks, *up.shape), BF16),
         ],
         scratch_shapes=[
+            pltpu.VMEM((rows, width), F32),
+            pltpu.VMEM((2 * C, width), BF16),
+            pltpu.VMEM((2 * C, 2 * width), BF16),
+            pltpu.VMEM((2 * C, C), BF16),
             pltpu.VMEM((places, 2, rows // 8, C), BF16),
             pltpu.VMEM((8, C), F32),
+            pltpu.SemaphoreType.DMA((6,)),
             pltpu.VMEM(up.shape, BF16),
         ]
         + [pltpu.VMEM((rows, D), BF16)] * 4
@@ -391,7 +411,7 @@
         ]
         + ring_scratch(),
         compiler_params=pltpu.CompilerParams(
-            collective_id=0, has_side_effects=True, vmem_limit_bytes=44 << 20
+            collective_id=0, has_side_effects=True, vmem_limit_bytes=56 << 20
         ),
         cost_estimate=pl.CostEstimate(
             flops=60_000_000_000, bytes_accessed=40_000_000, transcendentals=0
@@ -400,7 +420,7 @@
     )(latent, turn, fine_a, fine_b, gain, w_query, w_key, w_value, w_in, up)
 
 
-def reduce_over_head(produce, meanwhile, term, taken, via_out, via_in, near, fin, send, recv):
+def reduce_over_head(produce, meanwhile, between, term, taken, via_out, via_in, near, fin, send, recv):
     _, y, c = seat()
     partner, up, down = 2 * y + 1 - c, 2 * plus(y, 1) + c, 2 * plus(y, 3) + c
 
@@ -413,13 +433,12 @@
     def pair(half, at):
         return term[half, at, c].astype(F32) + taken[half, at].astype(F32)
 
-    gives = []
-    for half in range(2):
-        produce(half)
-        gives.append(copy(term.at[half, :, 1 - c], taken.at[half], half, partner))
-        gives[half].start()
-    meanwhile()
     across, ahead, behind = plus(y, 2), plus(y, 1), plus(y, 3)
+    gives = [copy(term.at[half, :, 1 - c], taken.at[half], half, partner) for half in range(2)]
+    produce(0, 0)
+    produce(0, 1)
+    gives[0].start()
+    produce(1, 0)
     gives[0].wait_recv()
     via_out[0] = pair(0, across).astype(BF16)
     via_0 = copy(via_out.at[0], via_in.at[0], 2, up)
@@ -427,6 +446,9 @@
     near[1, 0] = pair(0, behind).astype(BF16)
     down_0 = copy(near.at[1, 0], fin.at[1, 0], 6, down)
     down_0.start()
+    produce(1, 1)
+    gives[1].start()
+    meanwhile()
     gives[1].wait_recv()
     via_out[1] = pair(1, across).astype(BF16)
     via_1 = copy(via_out.at[1], via_in.at[1], 3, down)
@@ -442,6 +464,7 @@
     near[1, 1] = (pair(1, behind) + via_in[1].astype(F32)).astype(BF16)
     down_1 = copy(near.at[1, 1], fin.at[1, 1], 7, down)
     down_1.start()
+    between()
     sums = [pair(half, y) for half in range(2)]
     down_0.wait_recv()
     up_0.wait_recv()
@@ -512,24 +535,31 @@
 
 
 def block_kernel(rows, heads, ringed, *refs):
-    (
-        x_ref, kv_ref, h_ref, n_ref, eq_ref, aq_ref, akv_ref, g_ref,
-        embedding_ref, win_ref, wo_ref, gain_ref, *refs,
-    ) = refs
+    kv_ref, *refs = refs
+    sources, refs = refs[:11], refs[11:]
     if ringed:
-        shard_ref, stream_ref, normed_out, full_ref, *refs = refs
+        shard_ref, stream_out, normed_out, full_ref, *refs = refs
         *refs, shard, load, local, gsend, grecv = refs
         ring = RingGather(shard, full_ref, local, gsend, grecv)
         fetch = pltpu.make_async_copy(shard_ref, shard, load)
     else:
-        stream_ref, normed_out, *refs = refs
-    normed_ref, queries, acc, sums, attended, *parts, send, recv = refs
+        stream_out, normed_out, *refs = refs
+    places, refs, loads = refs[:11], refs[12:], refs[11]
+    (
+        x_ref, h_ref, n_ref, eq_ref, aq_ref, akv_ref, g_ref,
+        win_ref, wo_ref, embedding_ref, gain_ref,
+    ) = places
+    inputs = staged(zip(sources, places), loads)
+    stream_ref, normed_ref, outs, queries, acc, sums, attended, *parts, send, recv = refs
     term = parts[0]
     share = rows // 8
     width = heads * HEAD_DIM
     block = pl.program_id(0)
     me, y, c = seat()
 
+    greeted = head_neighbours() + (ring.neighbours() if ringed else [])
+    results = staged([(stream_ref, stream_out), (normed_ref, normed_out)], outs)
+
     def scale_of(x, h, n):
         twice = jnp.concatenate([x, x], axis=1)
         quad = jnp.sum(x.astype(F32) * (dot(twice, g_ref[...]) + 2.0 * h), axis=1, keepdims=True)
@@ -539,10 +569,13 @@
     def _():
         if ringed:
             fetch.start()
-        greet(head_neighbours() + (ring.neighbours() if ringed else []))
+        each("start", inputs)
+        hail(greeted)
         if ringed:
+            met(greeted)
             fetch.wait()
             ring.begin()
+        each("wait", inputs[:7])
         own = pl.ds(pl.multiple_of(me * rows, rows), rows)
         twice, scale = scale_of(x_ref[own, :], h_ref[own, :], n_ref[own, :])
         value = (dot(twice, aq_ref[...]) + eq_ref[...]) * (scale * HEAD_DIM**-0.5)
@@ -583,16 +616,23 @@
     def _():
         step(True)
 
-    def produce(half):
-        for at in range(0, HALF, 768):
-            cols = slice(half * HALF + at, half * HALF + at + 768)
-            store_terms(term, half, at, share, dot(attended[...], wo_ref[:, cols]))
+    def produce(half, part):
+        at = part * (HALF // 2)
+        cols = slice(half * HALF + at, half * HALF + at + HALF // 2)
+        store_terms(term, half, at, share, dot(attended[...], wo_ref[:, cols]))
 
     def meanwhile():
         first = pl.ds(pl.multiple_of(me * rows + (2 * y + c) * share, share), share)
         stream_ref[...] = dot(x_ref[first, :], win_ref[...]) + embedding_ref[...]
+
+    def between():
         if ringed:
-            ring.first()
+            ring.second()
+            ring.middle()
+
+    def midway():
+        if ringed:
+            ring.third(2)
 
     @pl.when(block == pl.num_programs(0) - 1)
     def _():
@@ -600,16 +640,24 @@
             cols = slice(head * HEAD_DIM, (head + 1) * HEAD_DIM)
             total = jnp.sum(sums[:, cols], axis=1, keepdims=True)
             attended[:, cols] = (acc[:, cols] / total).astype(BF16)
-        total = reduce_over_head(produce, meanwhile, *parts)
+        each("wait", inputs[7:])
+        if ringed:
+            ring.first()
+        else:
+            met(greeted)
+        total = reduce_over_head(produce, meanwhile, between, *parts)
         stream = stream_ref[...] + total
         stream_ref[...] = stream
+        results[0].start()
         normed_ref[y, c] = layer_norm(stream, gain_ref[...]).astype(BF16)
-        gather_over_head(normed_ref, send, recv, ring.second if ringed else lambda: None)
-        normed_out[...] = normed_ref[...]
         if ringed:
-            ring.third()
-            ring.fourth()
+            ring.third(1)
+        gather_over_head(normed_ref, send, recv, midway)
+        results[1].start()
+        if ringed:
+            ring.third(3)
             ring.end()
+        each("wait", results)
 
 
 def block_step(rows, state, x, embedding, w_in, w_attn_out, gain, shard=None):
@@ -617,10 +665,10 @@
     length, width = kv.shape[0], kv.shape[1] // 2
     share = rows // 8
     ringed = shard is not None
-    whole = pl.BlockSpec(memory_space=pltpu.VMEM)
-    far = pl.BlockSpec(memory_space=pl.ANY)
+    far = pl.BlockSpec(memory_space=pltpu.HBM)
     tile = pl.BlockSpec((KEY_BLOCK, 2 * width), lambda i: (i, 0))
     more = [shard] if ringed else []
+    sources = [x, *state[1:], w_in, w_attn_out, embedding, gain]
     outs = [
         jax.ShapeDtypeStruct((share, D), F32),
         jax.ShapeDtypeStruct((4, 2, share, D), BF16),
@@ -630,11 +678,15 @@
     return pl.pallas_call(
         functools.partial(block_kernel, rows, width // HEAD_DIM, ringed),
         grid=(length // KEY_BLOCK,),
-        in_specs=[whole, tile] + [whole] * 10 + [far] * ringed,
-        out_specs=[whole] * 2 + [far] * ringed,
+        in_specs=[tile] + [far] * (11 + ringed),
+        out_specs=[far] * (2 + ringed),
         out_shape=outs,
-        scratch_shapes=[
+        scratch_shapes=[buffer_like(source) for source in sources]
+        + [
+            pltpu.SemaphoreType.DMA((11,)),
+            pltpu.VMEM((share, D), F32),
             pltpu.VMEM((4, 2, share, D), BF16),
+            pltpu.SemaphoreType.DMA((2,)),
             pltpu.VMEM((rows, width), BF16),
             pltpu.VMEM((rows, width), F32),
             pltpu.VMEM((rows, width), F32),
@@ -644,19 +696,21 @@
         + [pltpu.SemaphoreType.DMA((9,)), pltpu.SemaphoreType.DMA((9,))]
         + ([pltpu.VMEM(shard.shape, BF16), pltpu.SemaphoreType.DMA] + ring_scratch() if ringed else []),
         compiler_params=pltpu.CompilerParams(
-            collective_id=1 if ringed else 4, has_side_effects=True, vmem_limit_bytes=40 << 20
+            collective_id=1 if ringed else 4, has_side_effects=True, vmem_limit_bytes=56 << 20
         ),
         cost_estimate=pl.CostEstimate(
             flops=30_000_000_000, bytes_accessed=20_000_000, transcendentals=0
         ),
         name="block_ring" if ringed else "block",
-    )(x, *state, embedding, w_in, w_attn_out, gain, *more)
+    )(kv, *sources, *more)
 
 
 def mlp_kernel(
-    share, last, normed_ref, up_ref, down_ref, stream_ref, gain_ref, wf_ref, ahead_ref, out_ref,
-    up, down, hidden, loads, *scratch,
+    share, last, up_ref, down_ref, *refs,
 ):
+    sources, out_ref, refs = refs[:5], refs[5], refs[6:]
+    places, (up, down, hidden, loads, smalls, *scratch) = refs[:5], refs[5:]
+    normed_ref, stream_ref, gain_ref, wf_ref, ahead_ref = places
     *parts, send, recv = scratch
     term = parts[0]
     seq, y, c = seat()
@@ -671,20 +725,25 @@
         )
         for k in range(downs)
     ]
-    for fetch in fetches:
-        fetch.start()
+    inputs = staged(zip(sources, places), smalls)
+    inputs[0].start()
+    each("start", fetches)
+    each("start", inputs[1:])
+
+    def raise_hidden():
+        inputs[0].wait()
+        for k in range(ups):
+            fetches[k].wait()
+            pre = dot(normed_ref[...], up[k])
+            hidden[:, k * wide : (k + 1) * wide] = jax.nn.gelu(pre, approximate=True).astype(BF16)
+
     if last:
         mirror = lax.axis_size("seq") - 1 - seq
         sends_edge = jnp.logical_and(mirror > 0, 2 * y + c == 7)
         keeps_edge = jnp.logical_and(mirror - 1 == seq, 2 * y + c == 7)
         waits_edge = jnp.logical_and(mirror > 0, jnp.logical_not(keeps_edge))
         barrier = pltpu.get_barrier_semaphore()
-        for target in head_neighbours():
-            pl.semaphore_signal(barrier, inc=1, device_id=target, device_id_type=MESH)
-        for head in range(8):
-            pl.semaphore_signal(
-                barrier, inc=1, device_id={"seq": mirror, "head": head}, device_id_type=MESH
-            )
+        hail(head_neighbours() + [{"seq": mirror, "head": head} for head in range(8)])
 
         @pl.when(waits_edge)
         def _():
@@ -692,6 +751,8 @@
                 barrier, inc=1, device_id={"seq": mirror - 1, "head": 7}, device_id_type=MESH
             )
 
+        raise_hidden()
+
         @pl.when(keeps_edge)
         def _():
             pl.semaphore_wait(barrier, 18)
@@ -705,20 +766,14 @@
             pl.semaphore_wait(barrier, 11)
 
     else:
-        greet_all(out_ref.shape[0])
-
-    for k in range(ups):
-        fetches[k].wait()
-        pre = dot(normed_ref[...], up[k])
-        hidden[:, k * wide : (k + 1) * wide] = jax.nn.gelu(pre, approximate=True).astype(BF16)
-
-    def produce(half):
-        for at in range(downs // 2):
-            k = half * (downs // 2) + at
-            fetches[ups + k].wait()
-            store_terms(term, half, at * tall, share, dot_t(hidden[...], down[k]))
-
-    total = reduce_over_head(produce, lambda: None, *parts)
+        greet_all(out_ref.shape[0], raise_hidden)
+
+    def produce(half, part):
+        k = half * (downs // 2) + part
+        fetches[ups + k].wait()
+        store_terms(term, half, part * tall, share, dot_t(hidden[...], down[k]))
+
+    total = reduce_over_head(produce, lambda: None, lambda: each("wait", inputs[1:]), *parts)
     normed = layer_norm(stream_ref[...] + total, gain_ref[...]).astype(BF16)
     params = dot(normed, wf_ref[...])
     following = ahead_ref[...] * jnp.exp(jnp.tanh(params[:, C:])) + params[:, :C]
@@ -791,28 +846,31 @@
 def mlp(share, places, last, normed, up, down, stream, gain, w_final, ahead):
     whole = pl.BlockSpec(memory_space=pltpu.VMEM)
     rows, width = normed.shape[0], up.shape[1]
+    sources = [normed, stream, gain, w_final, ahead]
     shape = (9, share, C) if last else (places, 2, share, C)
     return pl.pallas_call(
         functools.partial(mlp_kernel, share, last),
-        in_specs=[whole] + [pl.BlockSpec(memory_space=pl.ANY)] * 2 + [whole] * 4,
+        in_specs=[pl.BlockSpec(memory_space=pltpu.HBM)] * 7,
         out_specs=whole,
         out_shape=jax.ShapeDtypeStruct(shape, BF16),
-        scratch_shapes=[
+        scratch_shapes=[buffer_like(source) for source in sources]
+        + [
             pltpu.VMEM((3, D, width // 3), BF16),
             pltpu.VMEM((4, D // 4, width), BF16),
             pltpu.VMEM((rows, width), BF16),
             pltpu.SemaphoreType.DMA((7,)),
+            pltpu.SemaphoreType.DMA((5,)),
         ]
         + reduce_scratch(share)
         + [pltpu.SemaphoreType.DMA((16,)), pltpu.SemaphoreType.DMA((2,))],
         compiler_params=pltpu.CompilerParams(
-            collective_id=3 if last else 2, has_side_effects=True, vmem_limit_bytes=44 << 20
+            collective_id=3 if last else 2, has_side_effects=True, vmem_limit_bytes=56 << 20
         ),
         cost_estimate=pl.CostEstimate(
             flops=40_000_000_000, bytes_accessed=30_000_000, transcendentals=0
         ),
         name="mlp_last" if last else "mlp",
-    )(normed, up, down, stream, gain, w_final, ahead)
+    )(up, down, *sources)
 
 
 def per_device(

time: 256 us -> 251 us (0.980)
  local copies, waits for them, and re-layouts: 19 us -> 4.02 us
  other arithmetic: 3.79 us -> 8.62 us
  Pallas kernels: 233 us -> 237 us
    unnamed x56 -> x2, local copies, waits for them, and re-layouts: 18.5 us -> 0.01 us
    pallas_call x1, Pallas kernels: 70.8 us -> 74.8 us  [first_call(): pl.pallas_call(functools.partial(first_kernel, rows), grid=(blocks,), in_...]
    pallas_call x2, Pallas kernels: 90.9 us -> 93.8 us  [block_step(): pl.pallas_call(functools.partial(block_kernel, rows, width // HEAD_DIM, r...]
where the time goes in v1:
time: 251 us; the launch traced here: 250 us
  Pallas kernels  237 us (94%)
  other arithmetic  8.62 us (3%)
  local copies, waits for them, and re-layouts  4.02 us (2%)
    pallas_call x2, Pallas kernels, block_step(): pl.pallas_call(functools.partial(block_kernel, rows, width // HEAD_DIM, r...  93.8 us
    pallas_call x1, Pallas kernels, first_call(): pl.pallas_call(functools.partial(first_kernel, rows), grid=(blocks,), in_...  74.8 us
    pallas_call x2, Pallas kernels, mlp(): pl.pallas_call(functools.partial(mlp_kernel, share, last), in_specs=[pl.B...  68.9 us

profile of v1, /device:TPU:1, one launch (start us, length us, event | category | flops | bytes accessed | tf_op | source)
XLA Modules:
  0.0 250.2 jit_solution(404655045006106465)
XLA Ops:
  0.0 0.7 iota_multiply_fusion
  0.7 1.1 multiply_sine_fusion
  1.9 0.7 pad_maximum_fusion.4.fine_b
  2.6 0.8 copy.15.fine_a
  3.5 0.8 copy.14.turn_ref
  4.3 74.8 %first.1 = (f32[4096,768]{1,0:T(8,128)}, f32[4096,128]{1,0:T(8,128)}, f32[4096,1]{1,0:T(8,128)}, f32[256,384]{1,0:T(8,128)}, bf16[256,384]{1,0:T(8,128)(2,1)}, /...) custom-call(f32[256,128]{1,0:T(8,128)} %latent_ref.1, ...), custom_call_target="tpu_custom_call" | custom-call | flops 60000002048 | bytes 40000000 | tf_op jit(solution)/shard_map/first/pallas_call | solution.py:368
  79.1 0.8 multiply_sine_fusion.1
  79.9 0.8 pad_maximum_fusion.1.refs_10_
  80.7 0.0 copy-start
  80.7 57.0 %block_ring.1 = (f32[32,3072]{1,0:T(8,128)}, bf16[4,2,32,3072]{3,2,1,0:T(8,128)(2,1)}, bf16[16,2,96,1536]{3,2,1,0:T(8,128)(2,1)}) custom-call(f32[4096,768]{1,0:T(8,128)} %get-tuple-element.22.refs_0_, bf16[4096,128]{1,0:T(8,128)(2,1)} %bitcast.28, f32[4096,128]{1,0:T(8,128)} %get-tuple-element.23.refs_2_, f32[4096,1]{1,0:T(8,128)} %get-tuple-element.24.refs_3_, ...), custom_call_target="tpu_custom_call" | custom-call | flops 30000001024 | bytes 20000000 | tf_op jit(solution)/shard_map/block_ring/pallas_call | solution.py:678
  137.7 0.7 slice.47
  138.4 0.0 copy-done
  138.4 0.6 fusion.refs_4_
  139.0 33.2 %mlp.1 = bf16[64,2,32,128]{3,2,1,0:T(8,128)(2,1)} custom-call(bf16[3072,1536]{1,0:T(8,128)(2,1)} %bitcast.38, bf16[3072,1536]{1,0:T(8,128)(2,1)} %bitcast.40, bf16[256,3072]{1,0:T(8,128)(2,1)} %bitcast.42, f32[32,3072]{1,0:T(8,128)} %get-tuple-element.31.refs_1_, f32[1,3072]{1,0:T(1,128)} %bitcast.36, bf16[3072,256]{1,0:T(8,128)(2,1)} %refs_3_.3, ...), custom_call_target="tpu_custom_call" | custom-call | flops 40000000000 | bytes 30000000 | tf_op jit(solution)/shard_map/mlp/pallas_call | solution.py:851
  172.2 0.7 slice.58
  172.9 2.5 pad_maximum_fusion.refs_1_
  175.4 36.7 %block.1 = (f32[32,3072]{1,0:T(8,128)}, bf16[4,2,32,3072]{3,2,1,0:T(8,128)(2,1)}) custom-call(f32[4096,768]{1,0:T(8,128)} %get-tuple-element.22.refs_0_, bf16[4096,128]{1,0:T(8,128)(2,1)} %pad_maximum_fusion.refs_1_, f32[4096,128]{1,0:T(8,128)} %get-tuple-element.23.refs_2_, f32[4096,1]{1,0:T(8,128)} %get-tuple-element.24.refs_3_, ...), custom_call_target="tpu_custom_call" | custom-call | flops 30000001024 | bytes 20000000 | tf_op jit(solution)/shard_map/block/pallas_call | solution.py:678
  212.1 35.7 %mlp_last.1 = bf16[9,32,128]{2,1,0:T(8,128)(2,1)} custom-call(bf16[3072,1536]{1,0:T(8,128)(2,1)} %bitcast.39, bf16[3072,1536]{1,0:T(8,128)(2,1)} %bitcast.41, bf16[256,3072]{1,0:T(8,128)(2,1)} %bitcast.43, f32[32,3072]{1,0:T(8,128)} %get-tuple-element.34.refs_1_, f32[1,3072]{1,0:T(1,128)} %bitcast.37, bf16[3072,256]{1,0:T(8,128)(2,1)} %refs_3_.3, ...), custom_call_target="tpu_custom_call" | custom-call | flops 40000000000 | bytes 30000000 | tf_op jit(solution)/shard_map/mlp_last/pallas_call | solution.py:851
  247.8 0.7 broadcast_select_fusion
  248.5 0.8 slice.50
  249.4 0.1 rev.3
  249.5 0.7 convert_element_type.26
  (7 shorter events, 0.1 us)
Async XLA Ops:
  80.7 57.7 %copy-start = (f32[256,128]{1,0:T(8,128)S(1)}, f32[256,128]{1,0:T(8,128)}, u32[]{:S(2)}) copy-start(f32[256,128]{1,0:T(8,128)} %latent_ref.1) | copy-start | bytes 393220

commit v2 on v1

--- a/solution.py
+++ b/solution.py
@@ -76,7 +76,7 @@
     pl.semaphore_wait(pltpu.get_barrier_semaphore(), len(targets))
 
 
-def greet_all(devices, meanwhile=lambda: None):
+def hail_all(devices):
     seq, y, c = seat()
     place = seq * 4 + y
     barrier = pltpu.get_barrier_semaphore()
@@ -91,8 +91,51 @@
             device_id_type=MESH,
         )
 
-    meanwhile()
-    pl.semaphore_wait(barrier, devices)
+
+def start_peers(count):
+    seq, y, c = seat()
+    return (
+        [{"seq": lax.rem(seq + k, count)} for k in range(1, count)]
+        + [{"head": 2 * plus(y, k) + c} for k in range(1, 4)]
+        + [{"head": 2 * y + 1 - c}]
+    )
+
+
+def start_spread(buffer, send, recv):
+    seq, y, c = seat()
+    count = buffer.shape[0]
+
+    def copy(block, slot, device):
+        return pltpu.make_async_remote_copy(
+            src_ref=block, dst_ref=block, send_sem=send.at[slot], recv_sem=recv.at[slot],
+            device_id=device, device_id_type=MESH,
+        )
+
+    partner = {"head": 2 * y + 1 - c}
+    plane = copy(buffer.at[pl.ds(0, count - 1), 0, c], 0, partner)
+    column = copy(buffer.at[:, pl.ds(0, 3), c], 1, partner)
+    across = copy(buffer.at[:, :, c], 2, partner)
+
+    def begin():
+        @pl.loop(1, count)
+        def _(k):
+            copy(buffer.at[seq, y, c], 0, {"seq": lax.rem(seq + k, count)}).start()
+
+    def columns():
+        plane.wait_recv()
+        for k in range(1, 4):
+            copy(buffer.at[:, y, c], 1, {"head": 2 * plus(y, k) + c}).start()
+
+    def cross():
+        column.wait_recv()
+        across.start()
+
+    def end():
+        plane.wait_send()
+        column.wait_send()
+        across.wait()
+
+    return begin, columns, cross, end
 
 
 def spread(buffer, send, recv):
@@ -215,10 +258,10 @@
         pltpu.make_async_copy(ref, wkv.at[:, pl.ds(k * width, width)], loads.at[k])
         for k, ref in enumerate((wk_ref, wv_ref))
     ]
-    begin, cross, end = spread(x_ref, xsend, xrecv)
+    begin, columns, cross, end = start_spread(x_ref, xsend, xrecv)
     count = lax.axis_size("seq")
     edge = pltpu.make_async_remote_copy(
-        src_ref=edge_rows, dst_ref=edge_ref, send_sem=xsend.at[2], recv_sem=xrecv.at[2],
+        src_ref=edge_rows, dst_ref=edge_ref, send_sem=xsend.at[3], recv_sem=xrecv.at[3],
         device_id={"seq": lax.rem(seq + count - 1, count)}, device_id_type=MESH,
     )
     ring = RingGather(shard, full_ref, local, gsend, grecv)
@@ -248,11 +291,12 @@
                 total = total + jnp.sum(part, axis=1, keepdims=True)
         mean[...] = total * (1.0 / D)
 
-    def tables():
+    def rows_out():
         edge_rows[...] = latent_ref[0:8, :]
         own = pl.ds(pl.multiple_of((2 * y + c) * (rows // 8), rows // 8), rows // 8)
-        x_ref[seq * 4 + y, c] = latent_ref[own, :].astype(BF16)
-
+        x_ref[seq, y, c] = latent_ref[own, :].astype(BF16)
+
+    def tables():
         @pl.loop(0, rows // 16)
         def _(k):
             sin_a, cos_a = fine_a[k, 0:1, :], fine_a[k, 1:2, :]
@@ -266,7 +310,7 @@
         high = gain.astype(BF16).astype(F32)
         line = lax.broadcasted_iota(jnp.int32, (16, D), 0)
         both = jnp.where(line == 0, high, jnp.where(line == 1, gain - high, 0.0)).astype(BF16)
-        for fetch in fetches:
+        for fetch in fetches[:2]:
             fetch.wait()
         gw[:, 0:width] = dot(both, wq_ref[...])
         gw[:, width:] = dot(both, wkv[...])
@@ -274,12 +318,18 @@
 
     @pl.when(step == 0)
     def _():
-        for fetch in fetches:
+        fetches[2].start()
+        peers = start_peers(count)
+        hail(peers)
+        rows_out()
+        for fetch in fetches[:2]:
             fetch.start()
-        greet_all(x_ref.shape[0], tables)
+        fetches[2].wait()
+        met(peers)
+        ring.begin()
         begin()
         edge.start()
-        ring.begin()
+        tables()
         fill(0, scaled_0, high_0, mean_0)
 
     def work(scaled, high, mean, others):
@@ -303,13 +353,12 @@
     def _():
         work(*odd, even)
 
-    @pl.when(step == 3)
-    def _():
-        cross()
-
-    for at, event in ((4, ring.first), (7, ring.second), (8, ring.middle)):
+    pl.when(step == 3)(columns)
+    pl.when(step == 6)(cross)
+
+    for at, event in ((3, ring.first), (7, ring.second), (9, ring.middle)):
         pl.when(step == at)(event)
-    for at, block in ((11, 1), (14, 2)):
+    for at, block in ((12, 1), (15, 2)):
         pl.when(step == at)(functools.partial(ring.third, block))
 
     @pl.when(step == steps - 1)
@@ -383,7 +432,7 @@
             jax.ShapeDtypeStruct((2 * C, width), BF16),
             jax.ShapeDtypeStruct((2 * C, 2 * width), BF16),
             jax.ShapeDtypeStruct((2 * C, C), BF16),
-            jax.ShapeDtypeStruct((places, 2, rows // 8, C), BF16),
+            jax.ShapeDtypeStruct((blocks, 4, 2, rows // 8, C), BF16),
             jax.ShapeDtypeStruct((8, C), F32),
             jax.ShapeDtypeStruct((blocks, *up.shape), BF16),
         ],
@@ -392,7 +441,7 @@
             pltpu.VMEM((2 * C, width), BF16),
             pltpu.VMEM((2 * C, 2 * width), BF16),
             pltpu.VMEM((2 * C, C), BF16),
-            pltpu.VMEM((places, 2, rows // 8, C), BF16),
+            pltpu.VMEM((blocks, 4, 2, rows // 8, C), BF16),
             pltpu.VMEM((8, C), F32),
             pltpu.SemaphoreType.DMA((6,)),
             pltpu.VMEM(up.shape, BF16),
@@ -406,8 +455,8 @@
             pltpu.VMEM((16, C), F32),
             pltpu.VMEM((8, C), F32),
             pltpu.SemaphoreType.DMA((3,)),
-            pltpu.SemaphoreType.DMA((3,)),
-            pltpu.SemaphoreType.DMA((3,)),
+            pltpu.SemaphoreType.DMA((4,)),
+            pltpu.SemaphoreType.DMA((4,)),
         ]
         + ring_scratch(),
         compiler_params=pltpu.CompilerParams(
@@ -534,31 +583,47 @@
         term[half, block // 2, block % 2, :, at : at + value.shape[1]] = rows
 
 
-def block_kernel(rows, heads, ringed, *refs):
+def layer_kernel(rows, heads, last, *refs):
+    ringed = not last
     kv_ref, *refs = refs
-    sources, refs = refs[:11], refs[11:]
+    sources, up_ref, down_ref, out, refs = refs[:14], refs[14], refs[15], refs[16], refs[17:]
     if ringed:
-        shard_ref, stream_out, normed_out, full_ref, *refs = refs
+        full_ref, *refs = refs
+    places, refs = refs[:14], refs[14:]
+    loads, landing, stream_ref, normed_ref, queries, acc, sums, attended, *refs = refs
+    up, down, hidden, wloads, msend, mrecv, *refs = refs
+    if ringed:
         *refs, shard, load, local, gsend, grecv = refs
         ring = RingGather(shard, full_ref, local, gsend, grecv)
-        fetch = pltpu.make_async_copy(shard_ref, shard, load)
-    else:
-        stream_out, normed_out, *refs = refs
-    places, refs, loads = refs[:11], refs[12:], refs[11]
+        fetch = pltpu.make_async_copy(down_ref, shard, load)
+        down_ref = full_ref
+    *parts, send, recv = refs
     (
         x_ref, h_ref, n_ref, eq_ref, aq_ref, akv_ref, g_ref,
-        win_ref, wo_ref, embedding_ref, gain_ref,
+        win_ref, wo_ref, embedding_ref, gain_ref, last_gain_ref, wf_ref, ahead_ref,
     ) = places
     inputs = staged(zip(sources, places), loads)
-    stream_ref, normed_ref, outs, queries, acc, sums, attended, *parts, send, recv = refs
+    wide = up.shape[2]
+    ups = [
+        pltpu.make_async_copy(up_ref.at[:, pl.ds(k * wide, wide)], up.at[k], wloads.at[k])
+        for k in range(up.shape[0])
+    ]
+    downs = [
+        pltpu.make_async_copy(
+            down_ref.at[pl.ds(k * 4, 4)], down.at[k], wloads.at[up.shape[0] + k]
+        )
+        for k in range(down.shape[0])
+    ]
     term = parts[0]
     share = rows // 8
     width = heads * HEAD_DIM
     block = pl.program_id(0)
     me, y, c = seat()
-
-    greeted = head_neighbours() + (ring.neighbours() if ringed else [])
-    results = staged([(stream_ref, stream_out), (normed_ref, normed_out)], outs)
+    if last:
+        mirror = lax.axis_size("seq") - 1 - me
+        sends_edge = jnp.logical_and(mirror > 0, 2 * y + c == 7)
+        keeps_edge = jnp.logical_and(mirror - 1 == me, 2 * y + c == 7)
+        waits_edge = jnp.logical_and(mirror > 0, jnp.logical_not(keeps_edge))
 
     def scale_of(x, h, n):
         twice = jnp.concatenate([x, x], axis=1)
@@ -570,9 +635,16 @@
         if ringed:
             fetch.start()
         each("start", inputs)
-        hail(greeted)
-        if ringed:
-            met(greeted)
+        each("start", ups if ringed else ups + downs)
+        if last:
+            hail(head_neighbours() + [{"seq": mirror, "head": head} for head in range(8)])
+
+            @pl.when(waits_edge)
+            def _():
+                hail([{"seq": mirror - 1, "head": 7}])
+        else:
+            hail_all(landing.shape[0])
+            pl.semaphore_wait(pltpu.get_barrier_semaphore(), landing.shape[0])
             fetch.wait()
             ring.begin()
         each("wait", inputs[:7])
@@ -634,6 +706,12 @@
         if ringed:
             ring.third(2)
 
+    def produce_down(half, part):
+        k = 2 * half + part
+        downs[k].wait()
+        weight = down[k].reshape(D // 4, hidden.shape[1])
+        store_terms(term, half, part * (HALF // 2), share, dot_t(hidden[...], weight))
+
     @pl.when(block == pl.num_programs(0) - 1)
     def _():
         for head in range(heads):
@@ -644,233 +722,172 @@
         if ringed:
             ring.first()
         else:
-            met(greeted)
+            barrier = pltpu.get_barrier_semaphore()
+
+            @pl.when(keeps_edge)
+            def _():
+                pl.semaphore_wait(barrier, 18)
+
+            @pl.when(jnp.logical_and(sends_edge, jnp.logical_not(keeps_edge)))
+            def _():
+                pl.semaphore_wait(barrier, 19)
+
+            @pl.when(jnp.logical_not(sends_edge))
+            def _():
+                pl.semaphore_wait(barrier, 11)
+
         total = reduce_over_head(produce, meanwhile, between, *parts)
         stream = stream_ref[...] + total
         stream_ref[...] = stream
-        results[0].start()
         normed_ref[y, c] = layer_norm(stream, gain_ref[...]).astype(BF16)
         if ringed:
             ring.third(1)
         gather_over_head(normed_ref, send, recv, midway)
-        results[1].start()
         if ringed:
             ring.third(3)
+        for k in range(up.shape[0]):
+            ups[k].wait()
+            pre = dot(normed_ref[...].reshape(rows, D), up[k])
+            hidden[:, k * wide : (k + 1) * wide] = jax.nn.gelu(pre, approximate=True).astype(BF16)
+        if ringed:
             ring.end()
-        each("wait", results)
-
-
-def block_step(rows, state, x, embedding, w_in, w_attn_out, gain, shard=None):
+            each("start", downs)
+        total = reduce_over_head(produce_down, lambda: None, lambda: None, *parts)
+        normed = layer_norm(stream_ref[...] + total, last_gain_ref[...]).astype(BF16)
+        params = dot(normed, wf_ref[...])
+        following = ahead_ref[...] * jnp.exp(jnp.tanh(params[:, C:])) + params[:, :C]
+        if last:
+            finish(following, landing, term, msend, mrecv)
+            out[...] = landing[...]
+        else:
+            landing[me * 4 + y, c] = following.astype(BF16)
+            begin, cross, end = spread(landing, msend, mrecv)
+            begin()
+            cross()
+            end()
+            before = x_ref[0:16, :].astype(F32)[0:1]
+            chunk = 8 * 2 * share
+            line = lax.broadcasted_iota(jnp.int32, (chunk, C), 0)
+            for k in range(landing.shape[0] // 8):
+                value = landing[8 * k : 8 * k + 8].reshape(chunk, C).astype(F32)
+                moved = jnp.where(line == 0, before, pltpu.roll(value, 1, 0))
+                out[k * chunk : (k + 1) * chunk, :] = moved.astype(BF16)
+                before = value[chunk - 1 :]
+
+
+def finish(following, out_ref, term, send, recv):
+    seq, y, c = seat()
+    mirror = lax.axis_size("seq") - 1 - seq
+    sends_edge = jnp.logical_and(mirror > 0, 2 * y + c == 7)
+    keeps_edge = jnp.logical_and(mirror - 1 == seq, 2 * y + c == 7)
+    waits_edge = jnp.logical_and(mirror > 0, jnp.logical_not(keeps_edge))
+    block = term.at[0, 0, 0, :, pl.ds(0, C)]
+    block[...] = following.astype(BF16)
+    head = 2 * y + c
+    moves = [
+        pltpu.make_async_remote_copy(
+            src_ref=block, dst_ref=out_ref.at[head], send_sem=send.at[k], recv_sem=recv.at[0],
+            device_id={"seq": mirror, "head": k}, device_id_type=MESH,
+        )
+        for k in range(8)
+    ]
+    edges = [
+        pltpu.make_async_remote_copy(
+            src_ref=block, dst_ref=out_ref.at[8], send_sem=send.at[8 + k], recv_sem=recv.at[1],
+            device_id={"seq": mirror - 1, "head": k}, device_id_type=MESH,
+        )
+        for k in range(8)
+    ]
+    for move in moves:
+        move.start()
+
+    @pl.when(sends_edge)
+    def _():
+        for move in edges[:7]:
+            move.start()
+
+    @pl.when(jnp.logical_and(sends_edge, jnp.logical_not(keeps_edge)))
+    def _():
+        edges[7].start()
+
+    whole = out_ref.at[pl.ds(0, 8)]
+    pltpu.make_async_remote_copy(
+        src_ref=whole, dst_ref=whole, send_sem=send.at[0], recv_sem=recv.at[0],
+        device_id={"seq": mirror, "head": 0}, device_id_type=MESH,
+    ).wait_recv()
+
+    @pl.when(waits_edge)
+    def _():
+        pltpu.make_async_remote_copy(
+            src_ref=block, dst_ref=out_ref.at[8], send_sem=send.at[0], recv_sem=recv.at[1],
+            device_id={"seq": mirror - 1, "head": 7}, device_id_type=MESH,
+        ).wait_recv()
+
+    for move in moves:
+        move.wait_send()
+
+    @pl.when(sends_edge)
+    def _():
+        for move in edges[:7]:
+            move.wait_send()
+
+    @pl.when(jnp.logical_and(sends_edge, jnp.logical_not(keeps_edge)))
+    def _():
+        edges[7].wait_send()
+
+    @pl.when(jnp.logical_not(waits_edge))
+    def _():
+        out_ref[8] = following.astype(BF16)
+
+
+def layer(rows, places, last, state, x, w_in, w_attn_out, embedding, gain, last_gain, w_final, ahead,
+          up, down):
     kv = state[0]
     length, width = kv.shape[0], kv.shape[1] // 2
-    share = rows // 8
-    ringed = shard is not None
+    share, hidden = rows // 8, up.shape[1]
+    count = length // rows
+    shard = (2, D // count // 2, hidden)
     far = pl.BlockSpec(memory_space=pltpu.HBM)
     tile = pl.BlockSpec((KEY_BLOCK, 2 * width), lambda i: (i, 0))
-    more = [shard] if ringed else []
-    sources = [x, *state[1:], w_in, w_attn_out, embedding, gain]
-    outs = [
-        jax.ShapeDtypeStruct((share, D), F32),
-        jax.ShapeDtypeStruct((4, 2, share, D), BF16),
-    ]
-    if ringed:
-        outs.append(jax.ShapeDtypeStruct((length // rows, *shard.shape), BF16))
+    sources = [x, *state[1:], w_in, w_attn_out, embedding, gain, last_gain, w_final, ahead]
+    shape = (9, share, C) if last else (places, 2, share, C)
+    outs = [jax.ShapeDtypeStruct(shape if last else (length, C), BF16)]
+    if not last:
+        outs.append(jax.ShapeDtypeStruct((count, *shard), BF16))
     return pl.pallas_call(
-        functools.partial(block_kernel, rows, width // HEAD_DIM, ringed),
+        functools.partial(layer_kernel, rows, width // HEAD_DIM, last),
         grid=(length // KEY_BLOCK,),
-        in_specs=[tile] + [far] * (11 + ringed),
-        out_specs=[far] * (2 + ringed),
+        in_specs=[tile] + [far] * 16,
+        out_specs=[pl.BlockSpec(memory_space=pltpu.VMEM)] + [far] * (not last),
         out_shape=outs,
         scratch_shapes=[buffer_like(source) for source in sources]
         + [
-            pltpu.SemaphoreType.DMA((11,)),
+            pltpu.SemaphoreType.DMA((14,)),
+            pltpu.VMEM(shape, BF16),
             pltpu.VMEM((share, D), F32),
             pltpu.VMEM((4, 2, share, D), BF16),
-            pltpu.SemaphoreType.DMA((2,)),
             pltpu.VMEM((rows, width), BF16),
             pltpu.VMEM((rows, width), F32),
             pltpu.VMEM((rows, width), F32),
             pltpu.VMEM((rows, width), BF16),
+            pltpu.VMEM((3, D, hidden // 3), BF16),
+            pltpu.VMEM((4, count // 4, *shard), BF16),
+            pltpu.VMEM((rows, hidden), BF16),
+            pltpu.SemaphoreType.DMA((7,)),
+            pltpu.SemaphoreType.DMA((16,)),
+            pltpu.SemaphoreType.DMA((2,)),
         ]
         + reduce_scratch(share)
         + [pltpu.SemaphoreType.DMA((9,)), pltpu.SemaphoreType.DMA((9,))]
-        + ([pltpu.VMEM(shard.shape, BF16), pltpu.SemaphoreType.DMA] + ring_scratch() if ringed else []),
+        + ([] if last else [pltpu.VMEM(shard, BF16), pltpu.SemaphoreType.DMA] + ring_scratch()),
         compiler_params=pltpu.CompilerParams(
-            collective_id=1 if ringed else 4, has_side_effects=True, vmem_limit_bytes=56 << 20
+            collective_id=2 if last else 1, has_side_effects=True, vmem_limit_bytes=60 << 20
         ),
         cost_estimate=pl.CostEstimate(
-            flops=30_000_000_000, bytes_accessed=20_000_000, transcendentals=0
+            flops=60_000_000_000, bytes_accessed=40_000_000, transcendentals=0
         ),
-        name="block_ring" if ringed else "block",
-    )(kv, *sources, *more)
-
-
-def mlp_kernel(
-    share, last, up_ref, down_ref, *refs,
-):
-    sources, out_ref, refs = refs[:5], refs[5], refs[6:]
-    places, (up, down, hidden, loads, smalls, *scratch) = refs[:5], refs[5:]
-    normed_ref, stream_ref, gain_ref, wf_ref, ahead_ref = places
-    *parts, send, recv = scratch
-    term = parts[0]
-    seq, y, c = seat()
-    ups, downs = up.shape[0], down.shape[0]
-    wide, tall = up.shape[2], down.shape[1]
-    fetches = [
-        pltpu.make_async_copy(up_ref.at[:, pl.ds(k * wide, wide)], up.at[k], loads.at[k])
-        for k in range(ups)
-    ] + [
-        pltpu.make_async_copy(
-            down_ref.at[pl.ds(k * tall, tall), :], down.at[k], loads.at[ups + k]
-        )
-        for k in range(downs)
-    ]
-    inputs = staged(zip(sources, places), smalls)
-    inputs[0].start()
-    each("start", fetches)
-    each("start", inputs[1:])
-
-    def raise_hidden():
-        inputs[0].wait()
-        for k in range(ups):
-            fetches[k].wait()
-            pre = dot(normed_ref[...], up[k])
-            hidden[:, k * wide : (k + 1) * wide] = jax.nn.gelu(pre, approximate=True).astype(BF16)
-
-    if last:
-        mirror = lax.axis_size("seq") - 1 - seq
-        sends_edge = jnp.logical_and(mirror > 0, 2 * y + c == 7)
-        keeps_edge = jnp.logical_and(mirror - 1 == seq, 2 * y + c == 7)
-        waits_edge = jnp.logical_and(mirror > 0, jnp.logical_not(keeps_edge))
-        barrier = pltpu.get_barrier_semaphore()
-        hail(head_neighbours() + [{"seq": mirror, "head": head} for head in range(8)])
-
-        @pl.when(waits_edge)
-        def _():
-            pl.semaphore_signal(
-                barrier, inc=1, device_id={"seq": mirror - 1, "head": 7}, device_id_type=MESH
-            )
-
-        raise_hidden()
-
-        @pl.when(keeps_edge)
-        def _():
-            pl.semaphore_wait(barrier, 18)
-
-        @pl.when(jnp.logical_and(sends_edge, jnp.logical_not(keeps_edge)))
-        def _():
-            pl.semaphore_wait(barrier, 19)
-
-        @pl.when(jnp.logical_not(sends_edge))
-        def _():
-            pl.semaphore_wait(barrier, 11)
-
-    else:
-        greet_all(out_ref.shape[0], raise_hidden)
-
-    def produce(half, part):
-        k = half * (downs // 2) + part
-        fetches[ups + k].wait()
-        store_terms(term, half, part * tall, share, dot_t(hidden[...], down[k]))
-
-    total = reduce_over_head(produce, lambda: None, lambda: each("wait", inputs[1:]), *parts)
-    normed = layer_norm(stream_ref[...] + total, gain_ref[...]).astype(BF16)
-    params = dot(normed, wf_ref[...])
-    following = ahead_ref[...] * jnp.exp(jnp.tanh(params[:, C:])) + params[:, :C]
-    if not last:
-        out_ref[seq * 4 + y, c] = following.astype(BF16)
-        begin, cross, end = spread(out_ref, send, recv)
-        begin()
-        cross()
-        end()
-    else:
-        block = scratch[0].at[0, 0, 0, :, pl.ds(0, C)]
-        block[...] = following.astype(BF16)
-        head = 2 * y + c
-        moves = [
-            pltpu.make_async_remote_copy(
-                src_ref=block, dst_ref=out_ref.at[head], send_sem=send.at[k], recv_sem=recv.at[0],
-                device_id={"seq": mirror, "head": k}, device_id_type=MESH,
-            )
-            for k in range(8)
-        ]
-        edges = [
-            pltpu.make_async_remote_copy(
-                src_ref=block, dst_ref=out_ref.at[8], send_sem=send.at[8 + k], recv_sem=recv.at[1],
-                device_id={"seq": mirror - 1, "head": k}, device_id_type=MESH,
-            )
-            for k in range(8)
-        ]
-        for move in moves:
-            move.start()
-
-        @pl.when(sends_edge)
-        def _():
-            for move in edges[:7]:
-                move.start()
-
-        @pl.when(jnp.logical_and(sends_edge, jnp.logical_not(keeps_edge)))
-        def _():
-            edges[7].start()
-
-        whole = out_ref.at[pl.ds(0, 8)]
-        pltpu.make_async_remote_copy(
-            src_ref=whole, dst_ref=whole, send_sem=send.at[0], recv_sem=recv.at[0],
-            device_id={"seq": mirror, "head": 0}, device_id_type=MESH,
-        ).wait_recv()
-
-        @pl.when(waits_edge)
-        def _():
-            pltpu.make_async_remote_copy(
-                src_ref=block, dst_ref=out_ref.at[8], send_sem=send.at[0], recv_sem=recv.at[1],
-                device_id={"seq": mirror - 1, "head": 7}, device_id_type=MESH,
-            ).wait_recv()
-
-        for move in moves:
-            move.wait_send()
-
-        @pl.when(sends_edge)
-        def _():
-            for move in edges[:7]:
-                move.wait_send()
-
-        @pl.when(jnp.logical_and(sends_edge, jnp.logical_not(keeps_edge)))
-        def _():
-            edges[7].wait_send()
-
-        @pl.when(jnp.logical_not(waits_edge))
-        def _():
-            out_ref[8] = following.astype(BF16)
-
-
-def mlp(share, places, last, normed, up, down, stream, gain, w_final, ahead):
-    whole = pl.BlockSpec(memory_space=pltpu.VMEM)
-    rows, width = normed.shape[0], up.shape[1]
-    sources = [normed, stream, gain, w_final, ahead]
-    shape = (9, share, C) if last else (places, 2, share, C)
-    return pl.pallas_call(
-        functools.partial(mlp_kernel, share, last),
-        in_specs=[pl.BlockSpec(memory_space=pltpu.HBM)] * 7,
-        out_specs=whole,
-        out_shape=jax.ShapeDtypeStruct(shape, BF16),
-        scratch_shapes=[buffer_like(source) for source in sources]
-        + [
-            pltpu.VMEM((3, D, width // 3), BF16),
-            pltpu.VMEM((4, D // 4, width), BF16),
-            pltpu.VMEM((rows, width), BF16),
-            pltpu.SemaphoreType.DMA((7,)),
-            pltpu.SemaphoreType.DMA((5,)),
-        ]
-        + reduce_scratch(share)
-        + [pltpu.SemaphoreType.DMA((16,)), pltpu.SemaphoreType.DMA((2,))],
-        compiler_params=pltpu.CompilerParams(
-            collective_id=3 if last else 2, has_side_effects=True, vmem_limit_bytes=56 << 20
-        ),
-        cost_estimate=pl.CostEstimate(
-            flops=40_000_000_000, bytes_accessed=30_000_000, transcendentals=0
-        ),
-        name="mlp_last" if last else "mlp",
-    )(up, down, *sources)
+        name="layer_last" if last else "layer",
+    )(kv, *sources, up, down)
 
 
 def per_device(
@@ -898,20 +915,16 @@
         jnp.concatenate([latent[1:], edge[:1]], axis=0), mine * share, share, 0
     )
     top = x[:1]
+    down = w_down.T.reshape(shape)
     for step_index in range(ITERS):
         last = step_index == ITERS - 1
-        stream, normed, *full = block_step(
-            rows, state, x, embedding, w_in, w_attn_out, gain_mlp[None, :],
-            w_down.T.reshape(shape) if step_index == 0 else None,
-        )
-        if step_index == 0:
-            down = full[0].reshape(D, w_up.shape[1])
-        following = mlp(
-            share, places, last, normed.reshape(rows, D), up, down, stream, gain_final[None, :],
-            w_final, ahead,
+        x, *full = layer(
+            rows, places, last, state, x, w_in, w_attn_out, embedding, gain_mlp[None, :],
+            gain_final[None, :], w_final, ahead, up, down,
         )
         if not last:
-            x = jnp.concatenate([top, following.reshape(length, C)[:-1]], axis=0)
+            down = full[0]
+    following = x
     edge = jnp.where(me == seq_count - 1, top, following[8, share - 1 :])
     result = jnp.concatenate([edge, following[:8].reshape(rows, C)[:-1]], axis=0)
     return result[::-1].astype(F32)

time: 251 us -> 239 us (0.952)
  Pallas kernels: 237 us -> 229 us
    pallas_call x1, Pallas kernels: 74.8 us -> 65.6 us  [first_call(): pl.pallas_call(functools.partial(first_kernel, rows), grid=(blocks,), in_...]
    pallas_call x4 -> x2, Pallas kernels: 163 us -> 163 us  [layer(): pl.pallas_call(functools.partial(layer_kernel, rows, width // HEAD_DIM, l...]
where the time goes in v2:
time: 239 us
  Pallas kernels  229 us (96%)
  other arithmetic  6.11 us (3%)
  local copies, waits for them, and re-layouts  4.24 us (2%)
    pallas_call x2, Pallas kernels, layer(): pl.pallas_call(functools.partial(layer_kernel, rows, width // HEAD_DIM, l...  163 us
    pallas_call x1, Pallas kernels, first_call(): pl.pallas_call(functools.partial(first_kernel, rows), grid=(blocks,), in_...  65.6 us

profile of v2, /device:TPU:1, one launch (start us, length us, event | category | flops | bytes accessed | tf_op | source)
XLA Modules:
  0.0 239.0 jit_solution(567647921064850759)
XLA Ops:
  0.0 0.7 iota_multiply_fusion
  0.7 0.9 slice.43
  1.7 0.8 multiply_sine_fusion.1
  2.4 0.8 pad_maximum_fusion.refs_10_
  3.2 1.1 multiply_sine_fusion
  4.4 0.7 pad_maximum_fusion.3.fine_b
  5.1 0.8 copy.15.fine_a
  5.9 0.8 copy.14.turn_ref
  6.8 65.6 %first.1 = (f32[4096,768]{1,0:T(8,128)}, f32[4096,128]{1,0:T(8,128)}, f32[4096,1]{1,0:T(8,128)}, f32[256,384]{1,0:T(8,128)}, bf16[256,384]{1,0:T(8,128)(2,1)}, /...) custom-call(f32[256,128]{1,0:T(8,128)} %latent_ref.1, ...), custom_call_target="tpu_custom_call" | custom-call | flops 60000002048 | bytes 40000000 | tf_op jit(solution)/shard_map/first/pallas_call | solution.py:417
  72.4 0.7 slice.44
  73.1 0.6 fusion.refs_14_
  73.7 90.0 %layer.1 = (bf16[4096,128]{1,0:T(8,128)(2,1)}, bf16[16,2,96,1536]{3,2,1,0:T(8,128)(2,1)}) custom-call(f32[4096,768]{1,0:T(8,128)} %get-tuple-element.18.refs_0_, bf16[4096,128]{1,0:T(8,128)(2,1)} %bitcast.22, f32[4096,128]{1,0:T(8,128)} %get-tuple-element.19.refs_2_, f32[4096,1]{1,0:T(8,128)} %get-tuple-element.20.refs_3_, ...), custom_call_target="tpu_custom_call" | custom-call | flops 60000002048 | bytes 40000000 | tf_op jit(solution)/shard_map/layer/pallas_call | solution.py:857
  163.7 73.0 %layer_last.1 = bf16[9,32,128]{2,1,0:T(8,128)(2,1)} custom-call(f32[4096,768]{1,0:T(8,128)} %get-tuple-element.18.refs_0_, bf16[4096,128]{1,0:T(8,128)(2,1)} %get-tuple-element.27.refs_1_, f32[4096,128]{1,0:T(8,128)} %get-tuple-element.19.refs_2_, f32[4096,1]{1,0:T(8,128)} %get-tuple-element.20.refs_3_, f32[256,384]{1,0:T(8,128)} %get-tuple-element.21.refs_4_, ...), custom_call_target="tpu_custom_call" | custom-call | flops 60000002048 | bytes 40000000 | tf_op jit(solution)/shard_map/layer_last/pallas_call | solution.py:857
  236.7 0.7 broadcast_select_fusion
  237.4 0.8 slice.46
  238.2 0.1 rev.3
  238.4 0.7 convert_element_type.26
  (6 shorter events, 0.1 us)

commit v3 on v2

--- a/solution.py
+++ b/solution.py
@@ -2,6 +2,7 @@
 
 import jax
 import jax.numpy as jnp
+import numpy as np
 from jax import lax
 from jax.experimental import pallas as pl
 from jax.experimental.pallas import tpu as pltpu
@@ -38,7 +39,7 @@
 
 
 def frequencies():
-    return jnp.exp(-jnp.log(10000.0) * 2.0 * jnp.arange(HALF).astype(F32) / D)
+    return np.exp(-np.log(10000.0) * 2.0 * np.arange(HALF) / D).astype(np.float32)[None, :]
 
 
 MESH = pl.DeviceIdType.MESH
@@ -246,9 +247,10 @@
 
 
 def first_kernel(
-    rows, latent_ref, turn_ref, fine_a, fine_b, gain_ref, wq_ref, wk_ref, wv_ref, win_ref, up_ref,
-    kv_ref, h_ref, n_ref, eq_out, aq_out, akv_out, g_out, x_out, edge_out, full_ref,
-    eq_ref, aq_ref, akv_ref, g_ref, x_ref, edge_ref, stores, shard, scaled_0, scaled_1, high_0, high_1, mean_0, mean_1, base, wkv, gw, wsum, edge_rows,
+    rows, latent_ref, freq_ref, gain_ref, wq_ref, wk_ref, wv_ref, win_ref, up_ref,
+    kv_ref, h_ref, n_ref, eq_out, aq_out, akv_out, g_out, x_out, ahead_out,
+    embedding_out, full_ref, eq_ref, aq_ref, akv_ref, g_ref, x_ref, ahead_ref, embedding_ref, stores,
+    edge_ref, turn_ref, fine_a, fine_b, shard, scaled_0, scaled_1, high_0, high_1, mean_0, mean_1, base, wkv, gw, wsum, edge_rows,
     loads, xsend, xrecv, local, gsend, grecv,
 ):
     step, steps = pl.program_id(0), pl.num_programs(0)
@@ -269,7 +271,7 @@
     results = staged(
         [
             (eq_ref, eq_out), (aq_ref, aq_out), (akv_ref, akv_out), (g_ref, g_out),
-            (x_ref, x_out), (edge_ref, edge_out),
+            (x_ref, x_out), (ahead_ref, ahead_out), (embedding_ref, embedding_out),
         ],
         stores,
     )
@@ -297,6 +299,17 @@
         x_ref[seq, y, c] = latent_ref[own, :].astype(BF16)
 
     def tables():
+        row = lax.broadcasted_iota(jnp.int32, (16, HALF), 0).astype(F32)
+        angle = row * freq_ref[...]
+        sines, cosines = jnp.sin(angle), jnp.cos(angle)
+        fine_b[0], fine_b[1] = sines, cosines
+        for table in (fine_a, turn_ref):
+            for _ in range(4):
+                sines, cosines = 2.0 * sines * cosines, cosines * cosines - sines * sines
+            for k in range(16):
+                table[k, 0:1, :] = sines[k : k + 1]
+                table[k, 1:2, :] = cosines[k : k + 1]
+
         @pl.loop(0, rows // 16)
         def _(k):
             sin_a, cos_a = fine_a[k, 0:1, :], fine_a[k, 1:2, :]
@@ -305,6 +318,12 @@
             base[0, into, :] = sin_a * cos_b + cos_a * sin_b
             base[1, into, :] = cos_a * cos_b - sin_a * sin_b
 
+        share = rows // 8
+        own = pl.ds(pl.multiple_of((2 * y + c) * share, share), share)
+        sin_a, cos_a = turn_ref[seq, 0:1, :], turn_ref[seq, 1:2, :]
+        sin_b, cos_b = base[0, own, :], base[1, own, :]
+        embedding_ref[:, 0:HALF] = sin_a * cos_b + cos_a * sin_b
+        embedding_ref[:, HALF:] = cos_a * cos_b - sin_a * sin_b
         wsum[...] = dot_t(jnp.ones((16, D), BF16), win_ref[...])
         gain = gain_ref[...]
         high = gain.astype(BF16).astype(F32)
@@ -383,6 +402,13 @@
         g_ref[C : 2 * C, :] = low
         end()
         edge.wait()
+        share = rows // 8
+        head = 2 * y + c
+        own = latent_ref[pl.ds(pl.multiple_of(head * share, share), share), :]
+        beyond = pl.multiple_of(jnp.minimum((head + 1) * share, rows - 8), 8)
+        beyond = jnp.where(head == 7, edge_ref[0:1, :], latent_ref[pl.ds(beyond, 8), :][0:1])
+        line = lax.broadcasted_iota(jnp.int32, (share, C), 0)
+        ahead_ref[...] = jnp.where(line == share - 1, beyond, pltpu.roll(own, share - 1, 0))
         each("start", results)
         ring.end()
         each("wait", results)
@@ -397,19 +423,6 @@
 
 
 def first(rows, blocks, places, latent, gain, w_query, w_key, w_value, w_in, up):
-    freq = frequencies()
-    scale = jnp.array([rows, 16.0, 1.0], F32)[:, None] * jnp.arange(16, dtype=F32)[None, :]
-    angles = scale[:, :, None] * freq[None, None, :]
-    sines, cosines = jnp.sin(angles), jnp.cos(angles)
-    turn = jnp.stack([sines[0], cosines[0]], axis=1)
-    fine_a = jnp.stack([sines[1], cosines[1]], axis=1)
-    fine_b = jnp.stack([sines[2], cosines[2]], axis=0)
-    return first_call(rows, blocks, places, latent, turn, fine_a, fine_b, gain, w_query, w_key,
-                      w_value, w_in, up)
-
-
-def first_call(rows, blocks, places, latent, turn, fine_a, fine_b, gain, w_query, w_key, w_value,
-               w_in, up):
     width = w_key.shape[1]
     length = rows * blocks
     whole = pl.BlockSpec(memory_space=pltpu.VMEM)
@@ -417,13 +430,13 @@
     return pl.pallas_call(
         functools.partial(first_kernel, rows),
         grid=(blocks,),
-        in_specs=[whole] * 6 + [far, far, whole, far],
+        in_specs=[whole] * 4 + [far, far, whole, far],
         out_specs=[
             pl.BlockSpec((rows, 2 * width), lambda i: (i, 0)),
             pl.BlockSpec((rows, C), lambda i: (i, 0)),
             pl.BlockSpec((rows, 1), lambda i: (i, 0)),
         ]
-        + [far] * 7,
+        + [far] * 8,
         out_shape=[
             jax.ShapeDtypeStruct((length, 2 * width), F32),
             jax.ShapeDtypeStruct((length, C), F32),
@@ -433,7 +446,8 @@
             jax.ShapeDtypeStruct((2 * C, 2 * width), BF16),
             jax.ShapeDtypeStruct((2 * C, C), BF16),
             jax.ShapeDtypeStruct((blocks, 4, 2, rows // 8, C), BF16),
-            jax.ShapeDtypeStruct((8, C), F32),
+            jax.ShapeDtypeStruct((rows // 8, C), F32),
+            jax.ShapeDtypeStruct((rows // 8, D), F32),
             jax.ShapeDtypeStruct((blocks, *up.shape), BF16),
         ],
         scratch_shapes=[
@@ -442,8 +456,13 @@
             pltpu.VMEM((2 * C, 2 * width), BF16),
             pltpu.VMEM((2 * C, C), BF16),
             pltpu.VMEM((blocks, 4, 2, rows // 8, C), BF16),
+            pltpu.VMEM((rows // 8, C), F32),
+            pltpu.VMEM((rows // 8, D), F32),
+            pltpu.SemaphoreType.DMA((7,)),
             pltpu.VMEM((8, C), F32),
-            pltpu.SemaphoreType.DMA((6,)),
+            pltpu.VMEM((16, 2, HALF), F32),
+            pltpu.VMEM((16, 2, HALF), F32),
+            pltpu.VMEM((2, 16, HALF), F32),
             pltpu.VMEM(up.shape, BF16),
         ]
         + [pltpu.VMEM((rows, D), BF16)] * 4
@@ -466,7 +485,7 @@
             flops=60_000_000_000, bytes_accessed=40_000_000, transcendentals=0
         ),
         name="first",
-    )(latent, turn, fine_a, fine_b, gain, w_query, w_key, w_value, w_in, up)
+    )(latent, jnp.asarray(frequencies()), gain, w_query, w_key, w_value, w_in, up)
 
 
 def reduce_over_head(produce, meanwhile, between, term, taken, via_out, via_in, near, fin, send, recv):
@@ -757,8 +776,13 @@
         params = dot(normed, wf_ref[...])
         following = ahead_ref[...] * jnp.exp(jnp.tanh(params[:, C:])) + params[:, :C]
         if last:
-            finish(following, landing, term, msend, mrecv)
-            out[...] = landing[...]
+            finish(following, x_ref[0:16, :][0:1], landing, term, msend, mrecv)
+            count = landing.shape[0] * share
+            line = lax.broadcasted_iota(jnp.int32, (rows, count), 0)
+            column = lax.broadcasted_iota(jnp.int32, (rows, count), 1)
+            source = jnp.where(line == rows - 1, count - 1, rows - 2 - line)
+            pick = jnp.where(column == source, 1.0, 0.0).astype(BF16)
+            out[...] = dot(pick, landing[...].reshape(count, C))
         else:
             landing[me * 4 + y, c] = following.astype(BF16)
             begin, cross, end = spread(landing, msend, mrecv)
@@ -775,7 +799,7 @@
                 before = value[chunk - 1 :]
 
 
-def finish(following, out_ref, term, send, recv):
+def finish(following, top, out_ref, term, send, recv):
     seq, y, c = seat()
     mirror = lax.axis_size("seq") - 1 - seq
     sends_edge = jnp.logical_and(mirror > 0, 2 * y + c == 7)
@@ -835,9 +859,13 @@
     def _():
         edges[7].wait_send()
 
-    @pl.when(jnp.logical_not(waits_edge))
+    @pl.when(keeps_edge)
     def _():
         out_ref[8] = following.astype(BF16)
+
+    @pl.when(mirror == 0)
+    def _():
+        out_ref[8] = jnp.broadcast_to(top.astype(F32), following.shape).astype(BF16)
 
 
 def layer(rows, places, last, state, x, w_in, w_attn_out, embedding, gain, last_gain, w_final, ahead,
@@ -851,7 +879,7 @@
     tile = pl.BlockSpec((KEY_BLOCK, 2 * width), lambda i: (i, 0))
     sources = [x, *state[1:], w_in, w_attn_out, embedding, gain, last_gain, w_final, ahead]
     shape = (9, share, C) if last else (places, 2, share, C)
-    outs = [jax.ShapeDtypeStruct(shape if last else (length, C), BF16)]
+    outs = [jax.ShapeDtypeStruct((rows, C), F32) if last else jax.ShapeDtypeStruct((length, C), BF16)]
     if not last:
         outs.append(jax.ShapeDtypeStruct((count, *shard), BF16))
     return pl.pallas_call(
@@ -895,26 +923,17 @@
     gain_attn, gain_mlp, gain_final,
 ):
     seq_count, head_count = lax.axis_size("seq"), lax.axis_size("head")
-    me, mine = lax.axis_index("seq"), lax.axis_index("head")
     rows = latent.shape[0]
-    share = rows // head_count
     length = rows * seq_count
     places = seq_count * head_count // 2
-    start = me * rows + mine * share
 
     shape = (2, w_up.shape[0] // 2, w_up.shape[1])
-    *state, gathered, edge, up = first(
+    *state, gathered, ahead, embedding, up = first(
         rows, seq_count, places, latent, gain_attn[None, :], w_query, w_key, w_value, w_in,
         w_up.reshape(shape),
     )
     up = up.reshape(D, w_up.shape[1])
     x = gathered.reshape(length, C)
-    angles = (start + jnp.arange(share)).astype(F32)[:, None] * frequencies()[None, :]
-    embedding = jnp.concatenate([jnp.sin(angles), jnp.cos(angles)], axis=1)
-    ahead = lax.dynamic_slice_in_dim(
-        jnp.concatenate([latent[1:], edge[:1]], axis=0), mine * share, share, 0
-    )
-    top = x[:1]
     down = w_down.T.reshape(shape)
     for step_index in range(ITERS):
         last = step_index == ITERS - 1
@@ -924,10 +943,7 @@
         )
         if not last:
             down = full[0]
-    following = x
-    edge = jnp.where(me == seq_count - 1, top, following[8, share - 1 :])
-    result = jnp.concatenate([edge, following[:8].reshape(rows, C)[:-1]], axis=0)
-    return result[::-1].astype(F32)
+    return x
 
 
 def solution(mesh):

time: 239 us -> 231 us (0.967)
  other arithmetic: 6.11 us -> 0 us
  local copies, waits for them, and re-layouts: 4.24 us -> 1.57 us
    slice x4 -> x0, local copies, waits for them, and re-layouts: 2.48 us -> none  [the longest x1 0.92 us: per_device(): latent[1:]]
where the time goes in v3:
time: 231 us; the launch traced here: 230 us
  Pallas kernels  229 us (99%)
    pallas_call x2, Pallas kernels, layer(): pl.pallas_call(functools.partial(layer_kernel, rows, width // HEAD_DIM, l...  163 us
    pallas_call x1, Pallas kernels, first(): pl.pallas_call(functools.partial(first_kernel, rows), grid=(blocks,), in_...  65.4 us

profile of v3, /device:TPU:1, one launch (start us, length us, event | category | flops | bytes accessed | tf_op | source)
XLA Modules:
  0.0 230.4 jit_solution(7762271937695090727)
XLA Ops:
  0.0 65.4 %first.1 = (f32[4096,768]{1,0:T(8,128)}, f32[4096,128]{1,0:T(8,128)}, f32[4096,1]{1,0:T(8,128)}, f32[256,384]{1,0:T(8,128)}, bf16[256,384]{1,0:T(8,128)(2,1)}, /...) custom-call(f32[256,128]{1,0:T(8,128)} %latent_ref.1, ...), custom_call_target="tpu_custom_call" | custom-call | flops 60000002048 | bytes 40000000 | tf_op jit(solution)/shard_map/first/pallas_call | solution.py:430
  65.4 90.3 %layer.1 = (bf16[4096,128]{1,0:T(8,128)(2,1)}, bf16[16,2,96,1536]{3,2,1,0:T(8,128)(2,1)}) custom-call(f32[4096,768]{1,0:T(8,128)} %get-tuple-element.18.refs_0_, bf16[4096,128]{1,0:T(8,128)(2,1)} %bitcast.18, f32[4096,128]{1,0:T(8,128)} %get-tuple-element.20.refs_2_, f32[4096,1]{1,0:T(8,128)} %get-tuple-element.21.refs_3_, ...), custom_call_target="tpu_custom_call" | custom-call | flops 60000002048 | bytes 40000000 | tf_op jit(solution)/shard_map/layer/pallas_call | solution.py:885
  155.7 73.1 %layer_last.1 = f32[256,128]{1,0:T(8,128)} custom-call(f32[4096,768]{1,0:T(8,128)} %get-tuple-element.18.refs_0_, bf16[4096,128]{1,0:T(8,128)(2,1)} %get-tuple-element.29.refs_1_, f32[4096,128]{1,0:T(8,128)} %get-tuple-element.20.refs_2_, f32[4096,1]{1,0:T(8,128)} %get-tuple-element.21.refs_3_, f32[256,384]{1,0:T(8,128)} %get-tuple-element.22.refs_4_, ...), custom_call_target="tpu_custom_call" | custom-call | flops 60000002048 | bytes 40000000 | tf_op jit(solution)/shard_map/layer_last/pallas_call | solution.py:885
  228.8 1.6 copy.15
